TPU v7x, 32 devices: a whole 2x2x4 slice. The times are simulated.
32 devices in a mesh: dp: 8 (over y, x, core), mp: 4 (over z).
Axes of the slice: x: 2, y: 2, z: 4, core: 2. Of those that a mesh axis runs over, the one named last changes fastest.
Arguments:
- layer_input: bfloat16 [16384, 1024], P(('dp', 'mp')), may hold values from -9 to 9
- segment_ids: int32 [8, 2048], P('dp'), may hold values from 0 to 10, as said below
- grad_out: bfloat16 [16384, 1024], P(('dp', 'mp')), may hold values from -6 to 6
- qkv_weight: bfloat16 [1024, 3, 1024], P('dp', None, 'mp'), may hold values from -0.1875 to 0.1875
- attn_weight: bfloat16 [1024, 1024], P('dp', 'mp'), may hold values from -3 to 3
- inner_weight: bfloat16 [1024, 2, 2624], P('dp', None, 'mp'), may hold values from -0.1875 to 0.1875
- outer_weight: bfloat16 [1024, 2624], P('dp', 'mp'), may hold values from -0.25 to 0.25
- attn_gain: float32 [1024], replicated, may hold values from 0.1 to 1.9
- mlp_gain: float32 [1024], replicated, may hold values from 0.1 to 1.9
Outputs:
- layer_output: bfloat16 [16384, 1024], P(('dp', 'mp'))
- input_grad: float32 [16384, 1024], P(('dp', 'mp'))
- qkv_grad: float32 [1024, 3, 1024], P('dp', None, 'mp')
- attn_grad: float32 [1024, 1024], P('dp', 'mp')
- inner_grad: float32 [1024, 2, 2624], P('dp', None, 'mp')
- outer_grad: float32 [1024, 2624], P('dp', 'mp')
- attn_gain_grad: float32 [1024], replicated
- mlp_gain_grad: float32 [1024], replicated
- rms_values: float32 [4], replicated
Inputs may be any that keep to these rules, and one draw needn't show every extreme that they name: `segment_ids`: along each sequence the numbers never fall; the nonzero ones count the documents from 1 at the sequence's start, each document of 200 to 2000 tokens; zeros fill the tail after the last document, if any. Some sequence holds 2048 // 200 documents.
All inputs are finite; a program needn't handle non-finite values.
Results may differ from a plain program's by a relative error of at most 0.018.
Values may be sent and summed in bfloat16 or wider, within the bound.
A program may use at most 192 MiB of HBM per device.

v0:
```python
import functools
import math

import jax
import jax.numpy as jnp
from jax import lax
from jax.experimental import pallas as pl
from jax.experimental.pallas import tpu as pltpu
from jax.sharding import PartitionSpec as P

HEAD_DIM = 64
NORM_EPS = 1e-05
ROPE_BASE = 160000.0
BIG = 1e30
LANES = 128
WAYS = 4
BF = jnp.bfloat16
F32 = jnp.float32
VMEM_LIMIT = 56 * 1024 * 1024


def dot_nn(a, b):
    return lax.dot_general(a, b, (((1,), (0,)), ((), ())), preferred_element_type=F32)


def dot_nt(a, b):
    return lax.dot_general(a, b, (((1,), (1,)), ((), ())), preferred_element_type=F32)


def dot_tn(a, b):
    return lax.dot_general(a, b, (((0,), (0,)), ((), ())), preferred_element_type=F32)


def norm_stats(values):
    centre = jnp.mean(values, axis=-1, keepdims=True)
    shifted = values - centre
    spread = jnp.mean(shifted * shifted, axis=-1, keepdims=True)
    scale = lax.rsqrt(spread + NORM_EPS)
    return shifted * scale, scale


def norm_back(vhat, scale, gain, grad):
    u = grad * gain
    mean_u = jnp.mean(u, axis=-1, keepdims=True)
    mean_uv = jnp.mean(u * vhat, axis=-1, keepdims=True)
    return scale * (u - mean_u - vhat * mean_uv)


def doc_positions(segment):
    length = segment.shape[0]
    places = jnp.arange(length, dtype=jnp.int32)
    before = jnp.concatenate([jnp.full((1,), -1, jnp.int32), segment[:-1]])
    starts = jnp.where(segment != before, places, jnp.zeros_like(places))
    return places - lax.cummax(starts, axis=0)


def swap_halves(values):
    lane = lax.broadcasted_iota(jnp.int32, values.shape, 1)
    first = lane % HEAD_DIM < HEAD_DIM // 2
    back = pltpu.roll(values, LANES - HEAD_DIM // 2, 1)
    ahead = pltpu.roll(values, HEAD_DIM // 2, 1)
    return jnp.where(first, back, ahead)


def choose(at, values):
    out = values[0]
    for i in range(1, len(values)):
        out = jnp.where(at == i, values[i], out)
    return out


def params():
    return pltpu.CompilerParams(vmem_limit_bytes=VMEM_LIMIT)


def cost(flops, mib):
    return pl.CostEstimate(flops=int(flops), bytes_accessed=int(mib * 2**20), transcendentals=0)


def call(kernel, scalars, grid, in_specs, out_specs, out_shape, scratch, estimate, name):
    spec = pltpu.PrefetchScalarGridSpec(
        num_scalar_prefetch=1,
        grid=grid,
        in_specs=in_specs,
        out_specs=out_specs,
        scratch_shapes=scratch,
    )
    return functools.partial(
        pl.pallas_call(
            kernel,
            grid_spec=spec,
            out_shape=out_shape,
            compiler_params=params(),
            cost_estimate=estimate,
            name=name,
        ),
        scalars,
    )


def full(shape):
    return pl.BlockSpec(shape, lambda i, s: (0,) * len(shape))


def shape_of(shape, dtype):
    return jax.ShapeDtypeStruct(shape, dtype)


def side_by_side(ref, *at):
    return jnp.concatenate([ref[(d, *at)] for d in range(ref.shape[0])], axis=-1)


STEP = 256


def table_piece(m, info, out):
    rows = info.shape[0]
    here = slice(m * rows, (m + 1) * rows)
    segment, position = info[:, 0:1], info[:, 1:2]
    lane = lax.broadcasted_iota(jnp.int32, (1, LANES), 1)
    half = HEAD_DIM // 2
    frequency = jnp.exp((lane % half).astype(F32) * (-2.0 * math.log(ROPE_BASE) / HEAD_DIM))
    angle = position * frequency
    sine = jnp.sin(angle)
    out.cosine[here, :] = jnp.cos(angle)
    out.sine[here, :] = jnp.where(lane % HEAD_DIM < half, -sine, sine)
    t = lane % HEAD_DIM
    same = segment == t.astype(F32)
    masked = jnp.where(same, 0.0, -BIG)
    out.qaux[here, :] = jnp.where(t >= 16, 0.0, masked).astype(BF)
    found = jnp.where(same, 1.0, 0.0)
    counted = jnp.where(t < 19, 1.0, 0.0)
    out.kaux[here, :] = jnp.where(t < 16, found, counted).astype(BF)
    out.live[here, :] = jnp.where(segment != 0.0, 1.0, 0.0)


def qkv_piece(m, x, gain, weight, out):
    rows = x.shape[0]
    here = slice(m * rows, (m + 1) * rows)
    vhat, unused = norm_stats(x.astype(F32))
    normed = (vhat * gain).astype(BF)
    out.normed[here, :] = normed
    flat = dot_nt(normed, weight)
    cosine, sine = out.cosine[here, :], out.sine[here, :]
    kaux = out.kaux[here, :]
    lane = lax.broadcasted_iota(jnp.int32, (rows, LANES), 1)
    for pair in range(flat.shape[1] // (3 * LANES)):
        q, k, v = [
            flat[:, at : at + LANES] for at in range(pair * 3 * LANES, (pair + 1) * 3 * LANES, LANES)
        ]
        q = (q * cosine + swap_halves(q) * sine).astype(BF)
        k = (k * cosine + swap_halves(k) * sine).astype(BF)
        out.q[pair, here, :] = q * jnp.asarray(HEAD_DIM**-0.5, BF)
        out.ka[pair, 0, here, :] = jnp.where(lane < HEAD_DIM, k, kaux)
        out.ka[pair, 1, here, :] = jnp.where(lane >= HEAD_DIM, k, kaux)
        out.v[pair, here, :] = v.astype(BF)


def attn_step(pair, step, out):
    tokens = out.v.shape[1]
    chunk = 512
    here = pl.ds(pl.multiple_of(step * STEP, STEP), STEP)
    lane = lax.broadcasted_iota(jnp.int32, (STEP, LANES), 1)
    t = lane % HEAD_DIM
    q = out.q[pair, here, :]
    qaux = out.qaux[here, :]
    live = out.live[here, :]
    outs = []
    for head in range(2):
        mine = (lane < HEAD_DIM) if head == 0 else (lane >= HEAD_DIM)
        qa = jnp.where(mine, q, qaux)
        top = None
        for at in range(0, tokens, chunk):
            s = dot_nt(qa, out.ka[pair, head, at : at + chunk, :])
            out.scores[:, at : at + chunk] = s
            part = jnp.max(s, axis=-1, keepdims=True)
            top = part if top is None else jnp.maximum(top, part)
        total = jnp.zeros((STEP, 1), F32)
        mixed = jnp.zeros((STEP, LANES), F32)
        for at in range(0, tokens, chunk):
            p = jnp.exp(out.scores[:, at : at + chunk] - top)
            total += jnp.sum(p, axis=-1, keepdims=True)
            mixed += dot_nn(p.astype(BF), out.v[pair, at : at + chunk, :])
        outs.append(mixed * (live / total))
        log_sum = jnp.where(live > 0, top + jnp.log(total), BIG)
        high = log_sum.astype(BF)
        rest = log_sum - high.astype(F32)
        mid = rest.astype(BF)
        low = (rest - mid.astype(F32)).astype(BF)
        aux = jnp.where(t == 16, -high, jnp.where(t == 17, -mid, jnp.where(t == 18, -low, qaux)))
        out.qa[pair, head, here, :] = jnp.where(mine, q, aux)
    out.o[pair, here, :] = jnp.where(lane < HEAD_DIM, outs[0], outs[1]).astype(BF)


class Kept:
    names = ("normed", "cosine", "sine", "qa", "ka", "v", "o", "q", "qaux", "kaux", "live", "scores")

    def __init__(self, refs):
        for name, ref in zip(self.names, refs):
            setattr(self, name, ref)


def kept_shapes(tokens, model, pairs):
    outs = [
        shape_of((tokens, model), BF),
        shape_of((tokens, LANES), F32),
        shape_of((tokens, LANES), F32),
        shape_of((pairs, 2, tokens, LANES), BF),
        shape_of((pairs, 2, tokens, LANES), BF),
        shape_of((pairs, tokens, LANES), BF),
        shape_of((pairs, tokens, LANES), BF),
    ]
    scratch = [
        pltpu.VMEM((pairs, tokens, LANES), BF),
        pltpu.VMEM((tokens, LANES), BF),
        pltpu.VMEM((tokens, LANES), BF),
        pltpu.VMEM((tokens, 1), F32),
        pltpu.VMEM((STEP, tokens), F32),
    ]
    return outs, scratch


def alone_kernel(x_ref, info_ref, gain_ref, w_ref, *refs):
    out = Kept(refs)
    for m in range(WAYS):
        table_piece(m, info_ref[m], out)
        qkv_piece(m, x_ref[m], gain_ref[...], side_by_side(w_ref), out)

    def body(step, carry):
        per = out.v.shape[1] // STEP
        attn_step(step // per, step % per, out)
        return carry

    lax.fori_loop(0, out.v.shape[0] * out.v.shape[1] // STEP, body, 0)


def alone_call(x, info, gain, weight, pairs):
    outs, scratch = kept_shapes(WAYS * x.shape[1], x.shape[2], pairs)
    return pl.pallas_call(
        alone_kernel,
        in_specs=[pl.BlockSpec(memory_space=pltpu.VMEM)] * 4,
        out_specs=[pl.BlockSpec(memory_space=pltpu.VMEM)] * len(outs),
        out_shape=outs,
        scratch_shapes=scratch,
        compiler_params=params(),
        name="forward",
    )(x, info, gain, weight)


def piece_block(m, rows, per):
    return pl.BlockSpec((rows, LANES), lambda i, s: (jnp.clip(i - per * m, 0, per - 1), 0))


def attn_bwd_kernel(s_ref, *refs):
    qa_ref, ka_ref, v_ref, o_ref, do_refs = refs[0], refs[1], refs[2], refs[3], refs[4:8]
    cosq_ref, sinq_ref, cosk_ref, sink_ref = refs[8:12]
    out_refs = refs[12:16]
    va_ref, kt_ref, dk_acc, dv_acc = refs[16:20]
    step = pl.program_id(0)
    rows = do_refs[0].shape[0]
    chunk = v_ref.shape[0] // WAYS
    per = chunk // rows
    piece = step // per
    lane_k = lax.broadcasted_iota(jnp.int32, (chunk, LANES), 1)
    lane = lax.broadcasted_iota(jnp.int32, (rows, LANES), 1)
    zero = jnp.zeros((), BF)

    @pl.when(step == 0)
    def _():
        ones = jnp.where(lane_k % HEAD_DIM < 3, jnp.ones((), BF), zero)
        for m in range(WAYS):
            some = slice(m * chunk, (m + 1) * chunk)
            v = v_ref[some, :]
            for head in range(2):
                mine = (lane_k < HEAD_DIM) if head == 0 else (lane_k >= HEAD_DIM)
                va_ref[head, some, :] = jnp.where(mine, v, ones)
                own = jnp.where(mine, ka_ref[head, some, :], zero).astype(F32)
                kt_ref[head, :, some] = own.T.astype(BF)
        dk_acc[...] = jnp.zeros_like(dk_acc)
        dv_acc[...] = jnp.zeros_like(dv_acc)

    grad = choose(piece, [r[...] for r in do_refs])
    out = o_ref[...]
    product = grad.astype(F32) * out.astype(F32)
    turned = jnp.zeros((LANES, rows), F32)
    for head in range(2):
        mine = (lane < HEAD_DIM) if head == 0 else (lane >= HEAD_DIM)
        delta = jnp.sum(jnp.where(mine, product, 0.0), axis=-1, keepdims=True)
        high = delta.astype(BF)
        rest = delta - high.astype(F32)
        mid = rest.astype(BF)
        low = (rest - mid.astype(F32)).astype(BF)
        t = lane % HEAD_DIM
        aux = jnp.where(t == 0, -high, jnp.where(t == 1, -mid, jnp.where(t == 2, -low, zero)))
        grad_aug = jnp.where(mine, grad, aux)
        grad_own = jnp.where(mine, grad, zero)
        qa = qa_ref[head]
        q_own = jnp.where(mine, qa, zero)
        for m in range(WAYS):
            some = slice(m * chunk, (m + 1) * chunk)
            prob = jnp.exp(dot_nt(ka_ref[head, some, :], qa))
            back = dot_nt(va_ref[head, some, :], grad_aug)
            score_grad = (prob * back).astype(BF)
            dv_acc[some, :] += dot_nn(prob.astype(BF), grad_own)
            dk_acc[some, :] += dot_nn(score_grad, q_own)
            turned += dot_nn(kt_ref[head, :, some], score_grad)
    dq = turned.T * (HEAD_DIM**-0.5)
    dq = (dq * cosq_ref[...] - swap_halves(dq) * sinq_ref[...]).astype(BF)
    for m in range(WAYS):

        @pl.when(piece == m)
        def _(m=m):
            here = pl.ds(pl.multiple_of((step - m * per) * rows, rows), rows)
            out_refs[m][here, :LANES] = dq

    @pl.when(step == pl.num_programs(0) - 1)
    def _():
        for m in range(WAYS):
            some = slice(m * chunk, (m + 1) * chunk)
            dk = dk_acc[some, :]
            dk = dk * cosk_ref[some, :] - swap_halves(dk) * sink_ref[some, :]
            out_refs[m][:, LANES : 2 * LANES] = dk.astype(BF)
            out_refs[m][:, 2 * LANES :] = dv_acc[some, :].astype(BF)


def attn_bwd_call(scalars, qa, ka, v, grad, o, cosine, sine, pair):
    tokens = v.shape[1]
    chunk = tokens // WAYS
    rows = 256
    per = chunk // rows
    moving = [piece_block(m, rows, per) for m in range(WAYS)]
    block = pl.BlockSpec((rows, LANES), lambda i, s: (i, 0))
    return call(
        attn_bwd_kernel,
        scalars,
        (tokens // rows,),
        [
            pl.BlockSpec((None, 2, rows, LANES), lambda i, s: (pair, 0, i, 0)),
            pl.BlockSpec((None, 2, tokens, LANES), lambda i, s: (pair, 0, 0, 0)),
            pl.BlockSpec((None, tokens, LANES), lambda i, s: (pair, 0, 0)),
            pl.BlockSpec((None, rows, LANES), lambda i, s: (pair, i, 0)),
        ]
        + moving
        + [block, block, full((tokens, LANES)), full((tokens, LANES))],
        [full((chunk, 3 * LANES))] * WAYS,
        [shape_of((chunk, 3 * LANES), BF)] * WAYS,
        [
            pltpu.VMEM((2, tokens, LANES), BF),
            pltpu.VMEM((2, LANES, tokens), BF),
            pltpu.VMEM((tokens, LANES), F32),
            pltpu.VMEM((tokens, LANES), F32),
        ],
        cost(28 * tokens * tokens * LANES, 8),
        "attn_bwd",
    )(qa, ka, v, o, *grad, cosine, sine, cosine, sine)


def own_first(core, values):
    cut = [values[:, at : at + LANES] for at in range(0, values.shape[1], LANES)]
    turned = [cut[i ^ 1] for i in range(len(cut))]
    return jnp.where(core == 0, values, jnp.concatenate(turned, axis=-1))


MESH = pl.DeviceIdType.MESH
UP, DOWN, TO_X, TO_Y, TO_D, CORE_OWN, CORE_X, CORE_Y, CORE_D = range(9)
FROM_Z, FROM_X, FROM_Y, FROM_D = range(4)


class Place:
    def __init__(self):
        self.dp, self.z = lax.axis_index("dp"), lax.axis_index("mp")
        self.core, self.x, self.y = self.dp % 2, (self.dp // 2) % 2, self.dp // 4
        self.at_c = self.dp + 1 - 2 * self.core
        self.at_x = self.dp + 2 - 4 * self.x
        self.at_y = self.dp + 4 - 8 * self.y
        self.at_d = self.at_x + self.at_y - self.dp
        self.group = self.z // 2
        self.far_z = self.z + 2 - 4 * self.group
        self.quarter = self.z + self.core * (self.far_z - self.z)

    @staticmethod
    def mix(q, m):
        return (q + m) % 2 + 2 * ((q // 2 + m // 2) % 2)

    def stays(self, a, b):
        return jnp.logical_and(a == self.dp, b == self.z)

    def attention_of(self, m):
        h = self.mix(self.z, m)
        a, b = self.dp - self.core + (h // 2 + self.core) % 2, 2 * self.core + h % 2
        return a, b, self.stays(a, b)

    def owner_of(self, m):
        a, b = self.dp - self.core + self.group, self.mix(self.quarter, m)
        return a, b, self.stays(a, b)


def remote(src, dst, send, recv, device):
    return pltpu.make_async_remote_copy(
        src_ref=src, dst_ref=dst, send_sem=send, recv_sem=recv,
        device_id=device, device_id_type=MESH,
    )


class Move:
    def __init__(self, src, dst, send, recv, place):
        a, b, self.stays = place
        self.far = lambda: remote(src, dst, send, recv, (a, b))
        self.near = lambda: pltpu.make_async_copy(src, dst, recv)

    def start(self):
        pl.when(self.stays)(lambda: self.near().start())
        pl.when(jnp.logical_not(self.stays))(lambda: self.far().start())

    def wait_recv(self):
        self.far().wait_recv()

    def wait_send(self):
        pl.when(jnp.logical_not(self.stays))(lambda: self.far().wait_send())


def forward_kernel(x_ref, info_ref, gain_ref, qkv_ref, *refs, packs):
    parts, outs, heads_ref = refs[:packs], refs[packs : 2 * packs], refs[2 * packs]
    saved, refs = refs[2 * packs + 1 : 2 * packs + 7], refs[2 * packs + 7 :]
    qa, o, normed, cosine, sine, ka, v, q, qaux, kaux, live, scores = refs[:12]
    kept = Kept((normed, cosine, sine, qa, ka, v, o, q, qaux, kaux, live, scores))
    x_all, w_ref, infos = refs[12:15]
    (
        sends, recvs, cores, locals_, token_send, token_recv, head_send, head_recv,
        q_send, q_recv, save_sem,
    ) = refs[15:]
    dp, z = lax.axis_index("dp"), lax.axis_index("mp")
    core, xb, yb = dp % 2, (dp // 2) % 2, dp // 4
    at_c, at_x, at_y = dp + 1 - 2 * core, dp + 2 - 4 * xb, dp + 4 - 8 * yb
    at_d = at_x + at_y - dp
    group = z // 2
    far_z = z + 2 - 4 * group
    quarter = z + core * (far_z - z)

    def mix(q, m):
        return (q + m) % 2 + 2 * ((q // 2 + m // 2) % 2)

    def attention_of(m):
        h = mix(z, m)
        return dp - core + (h // 2 + core) % 2, 2 * core + h % 2

    def owner_of(m):
        return dp - core + group, mix(quarter, m)

    barrier = pltpu.get_barrier_semaphore()

    def greet(device, when=None):
        def signal():
            pl.semaphore_signal(barrier, inc=1, device_id=device, device_id_type=MESH)

        signal() if when is None else pl.when(when)(signal)

    greet((at_c, z))
    greet((at_x, z))
    greet((at_y, z))
    greet((dp, far_z))
    greet((dp, z + 1), z < WAYS - 1)
    greet((dp, z - 1), z > 0)
    count = 4 + (z < WAYS - 1).astype(jnp.int32) + (z > 0).astype(jnp.int32)
    here, there = [], []
    for m in range(WAYS):
        for of, found in ((attention_of, here), (owner_of, there)):
            a, b = of(m)
            stays = jnp.logical_and(a == dp, b == z)
            found.append((a, b, stays))
            greet((a, b), jnp.logical_not(stays))
            count += 1 - stays.astype(jnp.int32)
    pl.semaphore_wait(barrier, count)

    def remote(src, dst, send, recv, device):
        return pltpu.make_async_remote_copy(
            src_ref=src, dst_ref=dst, send_sem=send, recv_sem=recv,
            device_id=device, device_id_type=MESH,
        )

    def copy(p, kind, s, src=None):
        who = {CORE_X: at_x, CORE_Y: at_y, CORE_D: at_d}.get(kind, dp)
        if kind == TO_D:
            who = jnp.where(s < 2, at_x, at_y)
        slab = outs[p].at[who, s]
        send = sends.at[p, kind, s]
        if kind == UP:
            recv, device = recvs.at[p, FROM_Z, s], (dp, z + 1)
        elif kind == DOWN:
            recv, device = recvs.at[p, FROM_Z, s], (dp, z - 1)
        elif kind == TO_X:
            recv, device = recvs.at[p, FROM_X, s], (at_x, z)
        elif kind == TO_Y:
            recv, device = recvs.at[p, FROM_Y, s], (at_y, z)
        elif kind == TO_D:
            recv, device = recvs.at[p, FROM_D, s], (jnp.where(s < 2, at_y, at_x), z)
        else:
            recv, device = cores.at[p, kind - CORE_OWN, s], (at_c, z)
        return remote(slab if src is None else src, slab, send, recv, device)

    def arrived(p, sem, who, s):
        slab = outs[p].at[who, s]
        remote(slab, slab, sends.at[p, UP, s], sem, (at_c, z)).wait_recv()

    def spread(p, s, src=None):
        copy(p, TO_X, s, src).start()
        copy(p, TO_Y, s, src).start()
        copy(p, CORE_OWN, s, src).start()

    def begin(p):
        src = parts[p]
        spread(p, z, src)
        pltpu.make_async_copy(src, outs[p].at[dp, z], locals_.at[p]).start()

    def begin_line(p):
        src = parts[p]
        pl.when(z < WAYS - 1)(lambda: copy(p, UP, z, src).start())
        pl.when(z > 0)(lambda: copy(p, DOWN, z, src).start())

    def reach(p, hop):
        def one(s):
            arrived(p, recvs.at[p, FROM_Z, s], dp, s)
            spread(p, s)

        pl.when(z >= hop)(lambda: one(z - hop))
        pl.when(z + hop < WAYS)(lambda: one(z + hop))

    def ahead(p, hop):
        pl.when(jnp.logical_and(z >= hop, z < WAYS - 1))(lambda: copy(p, UP, z - hop).start())
        pl.when(jnp.logical_and(z + hop < WAYS, z > 0))(lambda: copy(p, DOWN, z + hop).start())

    def line(p, hop):
        reach(p, hop)
        if hop < WAYS - 1:
            ahead(p, hop)

    def plane(p, hop):
        def one(s):
            arrived(p, recvs.at[p, FROM_X, s], at_x, s)
            copy(p, CORE_X, s).start()
            pl.when(s < 2)(lambda: copy(p, TO_D, s).start())
            arrived(p, recvs.at[p, FROM_Y, s], at_y, s)
            copy(p, CORE_Y, s).start()
            pl.when(s >= 2)(lambda: copy(p, TO_D, s).start())

        if hop == 0:
            one(z)
        else:
            pl.when(z >= hop)(lambda: one(z - hop))
            pl.when(z + hop < WAYS)(lambda: one(z + hop))

    def corner(p, hop):
        def one(s):
            arrived(p, recvs.at[p, FROM_D, s], at_d, s)
            copy(p, CORE_D, s).start()

        if hop == 0:
            one(z)
        else:
            pl.when(z >= hop)(lambda: one(z - hop))
            pl.when(z + hop < WAYS)(lambda: one(z + hop))

    def from_core(p):
        for s in range(WAYS):
            for kind in range(4):
                twin = (at_c, at_x + at_c - dp, at_y + at_c - dp, at_d + at_c - dp)[kind]
                arrived(p, cores.at[p, kind, s], twin, s)
        pltpu.make_async_copy(parts[p], outs[p].at[dp, z], locals_.at[p]).wait()

    def finish(p):
        for s in range(WAYS):
            pl.when(jnp.logical_and(z < WAYS - 1, s <= z))(lambda s=s: copy(p, UP, s).wait_send())
            pl.when(jnp.logical_and(z > 0, s >= z))(lambda s=s: copy(p, DOWN, s).wait_send())
            for kind in range(TO_X, CORE_D + 1):
                copy(p, kind, s).wait_send()

    def token(m):
        to_dp, to_z, stays = here[m]

        def far():
            return remote(x_ref, x_all.at[m], token_send.at[m], token_recv.at[m], (to_dp, to_z))

        def near():
            return pltpu.make_async_copy(x_ref, x_all.at[m], token_recv.at[m])

        return far, near, stays

    def pass_on(m):
        return remote(
            x_all.at[m], x_all.at[m + 2], token_send.at[m + 2], token_recv.at[m + 2], (at_c, z)
        )

    def swap_info():
        return remote(info_ref, infos.at[1], token_send.at[WAYS], token_recv.at[WAYS], (at_c, z))

    def own_info():
        return pltpu.make_async_copy(info_ref, infos.at[0], locals_.at[packs])

    def q_copy(kind, i=0, src=None):
        who = {"z": dp, "x": dp, "y": dp, "c": dp, "cx": at_x, "cy": at_y, "cd": at_d}.get(kind)
        if kind == "d":
            who = at_x if i == 0 else at_y
        device = {"z": (dp, far_z), "x": (at_x, z), "y": (at_y, z)}.get(kind, (at_c, z))
        if kind == "d":
            device = (at_y, z) if i == 0 else (at_x, z)
        slot = {"z": 0, "x": 1, "y": 3, "d": 5, "c": 7, "cx": 8, "cy": 9, "cd": 10}[kind]
        if kind in ("x", "y", "d"):
            slot += i
        if kind == "z":
            i = 1
        if kind[0] == "c":
            i = 1 - core
        dst = w_ref.at[i, who]
        return remote(dst if src is None else src, dst, q_send.at[slot], q_recv.at[slot], device)

    def q_arrived(kind, i=0):
        q_copy(kind, i).wait_recv()

    def own_q():
        return pltpu.make_async_copy(qkv_ref, w_ref.at[0, dp], locals_.at[packs + 1])

    q_kinds = [("z", 0), ("x", 0), ("x", 1), ("y", 0), ("y", 1), ("d", 0), ("d", 1)]
    q_kinds += [("c", 0), ("cx", 0), ("cy", 0), ("cd", 0)]

    keeps = [w_ref.at[core], normed, cosine, sine, ka, v]

    def save(i):
        return pltpu.make_async_copy(keeps[i], saved[i], save_sem.at[i])

    rows = x_ref.shape[0]

    def head(pair, m, owner):
        src = kept.o.at[pair, pl.ds(m * rows, rows)]
        dst = heads_ref.at[m, pair]
        to_dp, to_z, stays = owner

        def far():
            return remote(
                src, dst, head_send.at[m, pair], head_recv.at[m, pair], (to_dp, to_z)
            )

        def near():
            return pltpu.make_async_copy(src, dst, head_recv.at[m, pair])

        return far, near, stays

    def start(item):
        far, near, stays = item
        pl.when(stays)(lambda: near().start())
        pl.when(jnp.logical_not(stays))(lambda: far().start())

    def end_send(item):
        far, near, stays = item
        pl.when(jnp.logical_not(stays))(lambda: far().wait_send())

    q_copy("z", 0, qkv_ref).start()
    q_copy("x", 0, qkv_ref).start()
    q_copy("y", 0, qkv_ref).start()
    own_q().start()
    for m in range(2):
        start(token(m))
    swap_info().start()
    own_info().start()
    for p in range(packs):
        begin(p)
        begin_line(p)
    own_info().wait()
    swap_info().wait()
    own_q().wait()
    q_arrived("x", 0)
    q_copy("d", 0).start()
    q_arrived("z")
    q_copy("x", 1).start()
    q_copy("y", 1).start()
    away = (group + core) % 2
    for m in range(WAYS):
        table_piece(m, infos[away, mix(quarter, m)], kept)
    q_arrived("y", 0)
    q_copy("c").start()
    plane(0, 0)
    q_arrived("x", 1)
    q_copy("cx").start()
    q_arrived("y", 1)
    q_copy("d", 1).start()
    q_copy("cy").start()
    plane(1, 0)
    q_arrived("d", 0)
    q_arrived("d", 1)
    q_copy("cd").start()
    reach(0, 1)
    corner(0, 0)
    reach(1, 1)
    corner(1, 0)
    for kind in ("c", "cx", "cy", "cd"):
        q_arrived(kind)
    save(0).start()
    save(2).start()
    save(3).start()
    for m in range(2):
        token(m)[0]().wait_recv()
        pass_on(m).start()
    for p in range(packs):
        ahead(p, 1)
        plane(p, 1)
    for m in range(WAYS):
        if m >= 2:
            pass_on(m - 2).wait_recv()
        weight = jnp.concatenate([w_ref[core, d] for d in range(w_ref.shape[1])], axis=-1)
        qkv_piece(m, x_all[m], gain_ref[...], weight, kept)
        if m == 2:
            line(0, 2)
            corner(0, 1)
    save(1).start()
    save(4).start()
    save(5).start()

    events = {
        1: [(line, 1, 2), (corner, 1, 1)],
        4: [(line, 0, 3), (plane, 0, 2)],
        7: [(line, 1, 3), (plane, 1, 2)],
        9: [(corner, 0, 2)],
        11: [(plane, 0, 3)],
        13: [(corner, 1, 2)],
    }
    steps = kept.v.shape[1] // STEP
    pairs = kept.v.shape[0]
    per = steps // WAYS

    def body(i, carry):
        for at, todo in events.items():

            @pl.when(i == at)
            def _(todo=todo):
                for what, p, hop in todo:
                    what(p, hop)

        pair = i // steps
        step = i % steps
        attn_step(pair, step, kept)
        m = step // per

        @pl.when(step % per == per - 1)
        def _():
            a, b = dp - core + group, mix(quarter, m)
            start(head(pair, m, (a, b, jnp.logical_and(a == dp, b == z))))

        return carry

    lax.fori_loop(0, pairs * steps, body, 0)
    plane(1, 3)
    corner(0, 3)
    corner(1, 3)
    for p in range(packs):
        from_core(p)
    for m in range(WAYS):
        for pair in range(pairs):
            head(pair, m, there[m])[0]().wait_recv()
            end_send(head(pair, m, there[m]))
    for m in range(2):
        pass_on(m).wait_send()
        end_send(token(m))
    for p in range(packs):
        finish(p)
    for kind, i in q_kinds:
        q_copy(kind, i).wait_send()
    for i in range(len(keeps)):
        save(i).wait()


def forward_call(x, info, gain, qkv_part, parts, dps, pairs):
    rows, model = x.shape
    packs = len(parts)
    anywhere = pl.BlockSpec(memory_space=pl.ANY)
    vmem = pl.BlockSpec(memory_space=pltpu.VMEM)
    outs, scratch = kept_shapes(WAYS * rows, model, pairs)
    normed, cosine, sine, qa, ka, v, o = outs
    hold = [normed, cosine, sine, ka, v]
    weight = (dps,) + qkv_part.shape
    out = pl.pallas_call(
        functools.partial(forward_kernel, packs=packs),
        in_specs=[anywhere, anywhere, vmem] + [anywhere] * (1 + packs),
        out_specs=[anywhere] * (packs + 7) + [vmem] * 2,
        out_shape=[shape_of((dps, WAYS) + part.shape, BF) for part in parts]
        + [shape_of((WAYS, pairs, rows, LANES), BF), shape_of(weight, BF)]
        + hold
        + [qa, o],
        scratch_shapes=[pltpu.VMEM(h.shape, h.dtype) for h in hold]
        + scratch
        + [
            pltpu.VMEM((WAYS, rows, model), BF),
            pltpu.VMEM((2,) + weight, BF),
            pltpu.VMEM((2, WAYS, rows, LANES), F32),
            pltpu.SemaphoreType.DMA((packs, 9, WAYS)),
            pltpu.SemaphoreType.DMA((packs, 4, WAYS)),
            pltpu.SemaphoreType.DMA((packs, 4, WAYS)),
            pltpu.SemaphoreType.DMA((packs + 2,)),
            pltpu.SemaphoreType.DMA((WAYS + 1,)),
            pltpu.SemaphoreType.DMA((WAYS + 1,)),
            pltpu.SemaphoreType.DMA((WAYS, pairs)),
            pltpu.SemaphoreType.DMA((WAYS, pairs)),
            pltpu.SemaphoreType.DMA((11,)),
            pltpu.SemaphoreType.DMA((11,)),
            pltpu.SemaphoreType.DMA((6,)),
        ],
        compiler_params=pltpu.CompilerParams(
            collective_id=0, has_side_effects=True, vmem_limit_bytes=VMEM_LIMIT
        ),
        name="forward",
    )(x, info, gain, qkv_part, *parts)
    packs_out, out = out[:packs], out[packs:]
    heads, weight, normed, cosine, sine, ka, v, qa, o = out
    return packs_out, heads, weight, (normed, cosine, sine, qa, ka, v, o)


def attn_back_begin(pair, k):
    chunk = 512
    lane = lax.broadcasted_iota(jnp.int32, (chunk, LANES), 1)
    zero = jnp.zeros((), BF)
    ones = jnp.where(lane % HEAD_DIM < 3, jnp.ones((), BF), zero)
    for at in range(0, k.dk.shape[0], chunk):
        some = slice(at, at + chunk)
        v = k.v[pair, some, :]
        for head in range(2):
            mine = (lane < HEAD_DIM) if head == 0 else (lane >= HEAD_DIM)
            k.va[head, some, :] = jnp.where(mine, v, ones)
            own = jnp.where(mine, k.ka[pair, head, some, :], zero).astype(F32)
            k.kt[head, :, some] = own.T.astype(BF)
    k.dk[...] = jnp.zeros_like(k.dk)
    k.dv[...] = jnp.zeros_like(k.dv)


def attn_back_step(pair, step, grad, k):
    chunk = 512
    here = pl.ds(pl.multiple_of(step * STEP, STEP), STEP)
    lane = lax.broadcasted_iota(jnp.int32, (STEP, LANES), 1)
    zero = jnp.zeros((), BF)
    t = lane % HEAD_DIM
    product = grad.astype(F32) * k.o[pair, here, :].astype(F32)
    turned = jnp.zeros((LANES, STEP), F32)
    for head in range(2):
        mine = (lane < HEAD_DIM) if head == 0 else (lane >= HEAD_DIM)
        delta = jnp.sum(jnp.where(mine, product, 0.0), axis=-1, keepdims=True)
        high = delta.astype(BF)
        rest = delta - high.astype(F32)
        mid = rest.astype(BF)
        low = (rest - mid.astype(F32)).astype(BF)
        aux = jnp.where(t == 0, -high, jnp.where(t == 1, -mid, jnp.where(t == 2, -low, zero)))
        grad_aug = jnp.where(mine, grad, aux)
        grad_own = jnp.where(mine, grad, zero)
        qa = k.qa[pair, head, here, :]
        q_own = jnp.where(mine, qa, zero)
        for at in range(0, k.dk.shape[0], chunk):
            some = slice(at, at + chunk)
            prob = jnp.exp(dot_nt(k.ka[pair, head, some, :], qa))
            back = dot_nt(k.va[head, some, :], grad_aug)
            score_grad = (prob * back).astype(BF)
            k.dv[some, :] += dot_nn(prob.astype(BF), grad_own)
            k.dk[some, :] += dot_nn(score_grad, q_own)
            turned += dot_nn(k.kt[head, :, some], score_grad)
    dq = turned.T * (HEAD_DIM**-0.5)
    dq = dq * k.cosine[here, :] - swap_halves(dq) * k.sine[here, :]
    k.low[pair, 0, here, :] = dq.astype(BF)


def attn_back_end(pair, k):
    chunk = 512
    for at in range(0, k.dk.shape[0], chunk):
        some = slice(at, at + chunk)
        dk = k.dk[some, :]
        dk = dk * k.cosine[some, :] - swap_halves(dk) * k.sine[some, :]
        k.low[pair, 1, some, :] = dk.astype(BF)
        k.low[pair, 2, some, :] = k.dv[some, :].astype(BF)


def low_piece(pair, m, k, rows):
    some = slice(m * rows, (m + 1) * rows)
    return jnp.concatenate([k.low[pair, c, some, :] for c in range(3)], axis=-1)


class Back:
    names = ("qa", "ka", "v", "o", "cosine", "sine", "low", "va", "kt", "dk", "dv")

    def __init__(self, refs):
        for name, ref in zip(self.names, refs):
            setattr(self, name, ref)


class Chain:
    def __init__(self, p, source, kept, r1, r2, rz, send, recv):
        self.p, self.source, self.kept = p, source, kept
        self.r1, self.r2, self.rz, self.send, self.recv = r1, r2, rz, send, recv

    def slab(self, q, slot, away):
        x, y = self.p.x, self.p.y
        if q < 2:
            return (y if slot else 1 - y) * 2 + (1 - x if away else x)
        return (1 - y if away else y) * 2 + (x if slot else 1 - x)

    def near(self, q, second=False):
        p = self.p
        return (p.at_x, p.z) if (q < 2) != second else (p.at_y, p.z)

    def stage1(self, q, slot):
        src = self.source(q, self.slab(q, slot, True))
        at = q * 2 + slot
        return remote(src, self.r1.at[q, slot], self.send.at[at], self.recv.at[at], self.near(q))

    def stage2(self, q):
        at = 8 + q
        src = self.kept(q, 0, self.slab(q, 0, False))
        return remote(src, self.r2.at[q], self.send.at[at], self.recv.at[at], self.near(q, True))

    def first(self, q):
        self.stage1(q, 0).start()
        self.stage1(q, 1).start()

    def second(self, q, done=False):
        if not done:
            self.stage1(q, 0).wait_recv()
        ref = self.kept(q, 0, self.slab(q, 0, False))
        ref[...] += self.r1[q, 0]
        self.stage2(q).start()
        if not done:
            self.stage1(q, 1).wait_recv()
        self.own(q)[...] += self.r1[q, 1]

    def own(self, q):
        return self.kept(q, 1, self.slab(q, 1, False))

    def third(self, q):
        self.stage2(q).wait_recv()
        self.own(q)[...] += self.r2[q]

    def lined(self, q, down):
        z = self.p.z
        at = q if down else q + 1
        return remote(
            self.own(q), self.rz.at[at], self.send.at[12 + q], self.recv.at[12 + at],
            (self.p.dp, z - 1 if down else z + 1),
        )

    def line(self, hop, quarters):
        z = self.p.z
        for q in quarters:
            if q < WAYS - hop:

                @pl.when(z == WAYS - hop)
                def _(q=q):
                    if hop > 1:
                        self.lined(q, True).wait_recv()
                        self.own(q)[...] += self.rz[q]
                    self.lined(q, True).start()

            if q > hop - 1:

                @pl.when(z == hop - 1)
                def _(q=q):
                    if hop > 1:
                        self.lined(q, False).wait_recv()
                        self.own(q)[...] += self.rz[q + 1]
                    self.lined(q, False).start()

    def last(self, out_ref):
        z = self.p.z
        for q in range(WAYS):

            @pl.when(z == q)
            def _(q=q):
                total = self.own(q)[...].astype(F32)
                if q < WAYS - 1:
                    self.lined(q, True).wait_recv()
                    total += self.rz[q].astype(F32)
                if q > 0:
                    self.lined(q, False).wait_recv()
                    total += self.rz[q + 1].astype(F32)
                out_ref[...] = total

    def finish(self, done=()):
        z = self.p.z
        for q in range(WAYS):
            if q not in done:
                self.stage1(q, 0).wait_send()
                self.stage1(q, 1).wait_send()
            self.stage2(q).wait_send()
            pl.when(q < z)(lambda q=q: self.lined(q, True).wait_send())
            pl.when(q > z)(lambda q=q: self.lined(q, False).wait_send())


DONE = (0, 2)


def turn_of(step):
    return 2 * (step % 2) + step // 2


def mlp_kernel(
    s_ref, heads_ref, x_ref, g_ref, gain_ref, live_ref, pack_ref, wa_ref, wb_ref,
    output_ref, mgrad_ref, low_ref, small_ref, hg_ref, sum_ref, r1_ref, *scratch, swap
):
    w_attn, middle, inner, mlp, back, grads, load_sem = scratch[:7]
    step = pl.program_id(0)
    steps = pl.num_programs(0)
    quarter = turn_of(step)
    units = wb_ref.shape[2] // 2
    skip = wa_ref.shape[2] - units
    z = s_ref[0]
    core = s_ref[1]
    load = pltpu.make_async_copy(pack_ref.at[:, :, :skip], w_attn, load_sem.at[0])
    if swap:
        away, got, send_sem, recv_sem, f_send, f_recv = scratch[7:]
        p = Place()
        core = p.core
        other = (p.at_c, p.z)
        chain = Chain(
            p, lambda q, i: grads.at[q, i], None, None, None, None, f_send, f_recv
        )

        @pl.when(step == 0)
        def _():
            barrier = pltpu.get_barrier_semaphore()
            for device in (other, (p.at_x, p.z), (p.at_y, p.z)):
                pl.semaphore_signal(barrier, inc=1, device_id=device, device_id_type=MESH)
            pl.semaphore_wait(barrier, 3)

        def give(i):
            return remote(
                away.at[i % 2], got.at[i % 2], send_sem.at[i % 2], recv_sem.at[i % 2], other
            )

        def stage1(i, slot):
            q = DONE[i]
            at = i * 2 + slot
            return remote(
                grads.at[q, chain.slab(q, slot, True)], r1_ref.at[i, slot],
                f_send.at[at], f_recv.at[at], chain.near(q),
            )

        def take(i):
            q = turn_of(i)
            give(i).wait_recv()
            for d in range(grads.shape[1]):
                grads[q, d] += got[i % 2, d]
            pltpu.make_async_copy(grads.at[q], sum_ref.at[q], load_sem.at[1 + i]).start()
            for j in range(len(DONE)):

                @pl.when(i == j)
                def _(j=j):
                    stage1(j, 0).start()
                    stage1(j, 1).start()

    @pl.when(step == 0)
    def _():
        load.start()
        tokens = x_ref[...].astype(F32)
        attn_out = jnp.zeros(tokens.shape, F32)
        load.wait()
        for m in range(WAYS):
            o = jnp.concatenate([heads_ref[m, 0], heads_ref[m, 1]], axis=-1)
            attn_out += dot_nn(o, side_by_side(w_attn, z ^ m))
        total = tokens + attn_out
        vhat, unused = norm_stats(total)
        middle[...] = total
        inner[...] = (vhat * gain_ref[...]).astype(BF)
        live = live_ref[...]
        lane = lax.broadcasted_iota(jnp.int32, (1, tokens.shape[1]), 1)
        sums = jnp.where(lane == 4, jnp.sum(live), 0.0)
        for i, values in enumerate((tokens, attn_out, total)):
            sums = jnp.where(lane == i, jnp.sum(live * values * values), sums)
        small_ref[...] = jnp.zeros_like(small_ref)
        small_ref[2:3, :] = sums

    w_act = side_by_side(wa_ref, 0, slice(skip, skip + units))
    w_lin = side_by_side(wb_ref, 0, slice(0, units))
    w_out = side_by_side(wb_ref, 0, slice(units, 2 * units))
    x = inner[...]
    grad = g_ref[...]
    act_in = dot_nt(w_act, x)
    linear = dot_nt(w_lin, x)
    hidden_grad = dot_nt(w_out, grad)
    cdf = 0.5 * (1.0 + lax.erf(act_in * (2.0**-0.5)))
    act = act_in * cdf
    slope = cdf + act_in * jnp.exp(-0.5 * act_in * act_in) * ((2.0 * math.pi) ** -0.5)
    hidden = (act * linear).astype(BF)
    d_act = (hidden_grad * linear * slope).astype(BF)
    d_lin = (hidden_grad * act).astype(BF)
    if swap:
        pl.when(step >= 1)(lambda: take(step - 1))
        pl.when(step >= 2)(lambda: give(step - 2).wait_send())
    x_mine = own_first(core, x)
    g_mine = own_first(core, grad)
    pieces = (dot_nn(d_act, x_mine), dot_nn(d_lin, x_mine), dot_nn(hidden, g_mine))
    for part, value in enumerate(pieces):
        some = slice(part * units, (part + 1) * units)
        value = value.astype(BF)
        for d in range(value.shape[1] // LANES):
            slab = value[:, d * LANES : (d + 1) * LANES]
            if not swap:
                sum_ref[quarter, d // 2, d % 2, some] = slab
            elif d % 2:
                away[step % 2, d // 2, some] = slab
            else:
                grads[quarter, d // 2, some] = slab
    if swap:
        give(step).start()
    more_mlp = dot_tn(hidden, w_out)
    more_back = dot_tn(d_act, w_act) + dot_tn(d_lin, w_lin)

    @pl.when(step == 0)
    def _():
        mlp[...] = more_mlp
        back[...] = more_back

    @pl.when(step > 0)
    def _():
        mlp[...] += more_mlp
        back[...] += more_back

    @pl.when(step == steps - 1)
    def _():
        if swap:
            take(step)
        vhat, scale = norm_stats(middle[...])
        into = back[...]
        middle_grad = g_ref[...].astype(F32) + norm_back(vhat, scale, gain_ref[...], into)
        low = middle_grad.astype(BF)
        for m in range(WAYS):
            hg = dot_nt(low, side_by_side(w_attn, z ^ m)).astype(BF)
            hg_ref[m, 0] = hg[:, :LANES]
            hg_ref[m, 1] = hg[:, LANES:]
        mgrad_ref[...] = middle_grad
        low_ref[...] = low
        out = mlp[...]
        output_ref[...] = (middle[...] + out).astype(BF)
        lane = lax.broadcasted_iota(jnp.int32, (1, out.shape[1]), 1)
        square = jnp.sum(live_ref[...] * out * out)
        small_ref[2:3, :] = jnp.where(lane == 3, square, small_ref[2:3, :])
        small_ref[1:2, :] = jnp.sum(into * vhat, axis=0, keepdims=True)
        if swap:
            give(step - 1).wait_send()
            give(step).wait_send()
            for i in range(WAYS):
                q = turn_of(i)
                pltpu.make_async_copy(grads.at[q], sum_ref.at[q], load_sem.at[1 + i]).wait()
            for i in range(len(DONE)):
                for slot in range(2):
                    stage1(i, slot).wait()


def mlp_call(scalars, heads, x, grad, gain, live, pack_a, pack_b, swap):
    tokens, model = x.shape
    wide, quarters, depth_a, unused = pack_a.shape
    units = pack_b.shape[2] // 2
    depth = model // WAYS
    out = (quarters, wide // 2) + (() if swap else (2,)) + (3 * units, LANES)
    whole = pl.BlockSpec(memory_space=pltpu.VMEM)
    anywhere = pl.BlockSpec(memory_space=pl.ANY)
    weight = lambda rows: pl.BlockSpec((wide, 1, rows, LANES), lambda i, s: (0, turn_of(i), 0, 0))
    sems = lambda *shape: pltpu.SemaphoreType.DMA(shape)
    scratch = [
        pltpu.VMEM((wide, quarters, depth, LANES), BF),
        pltpu.VMEM((tokens, model), F32),
        pltpu.VMEM((tokens, model), BF),
        pltpu.VMEM((tokens, model), F32),
        pltpu.VMEM((tokens, model), F32),
        pltpu.VMEM(out if swap else (8, LANES), BF),
        sems(1 + WAYS),
    ]
    if swap:
        scratch += [pltpu.VMEM((2,) + out[1:], BF)] * 2 + [sems(2), sems(2), sems(6), sems(6)]
    r1 = (len(DONE), 2, 3 * units, LANES) if swap else (8, LANES)
    spec = pltpu.PrefetchScalarGridSpec(
        num_scalar_prefetch=1,
        grid=(quarters,),
        in_specs=[whole] * 5 + [anywhere, weight(depth_a), weight(2 * units)],
        out_specs=[whole] * 5 + [anywhere if swap else whole, anywhere],
        scratch_shapes=scratch,
    )
    extra = dict(collective_id=1, has_side_effects=True) if swap else {}
    return pl.pallas_call(
        functools.partial(mlp_kernel, swap=swap),
        grid_spec=spec,
        out_shape=[
            shape_of((tokens, model), BF),
            shape_of((tokens, model), F32),
            shape_of((tokens, model), BF),
            shape_of((8, model), F32),
            shape_of((WAYS, depth // LANES, tokens, LANES), BF),
            shape_of(out, BF),
            shape_of(r1, BF),
        ],
        compiler_params=pltpu.CompilerParams(vmem_limit_bytes=62 * 1024 * 1024, **extra),
        cost_estimate=cost(22 * tokens * model * units * quarters, 40),
        name="mlp",
    )(scalars, heads, x, grad, gain, live, pack_a, pack_a, pack_b)


def backward_kernel(
    hg_ref, sum_ref, r1_ref, normed_ref, w_ref, x_ref, mgrad_ref, low_ref, heads_ref,
    qa, ka, v, o, cosine, sine, gain_ref, small_ref,
    grad_ref, ffn_ref, attn_ref, qkv_ref, total_ref,
    do_ref, low, va, kt, dk, dv, normed, weight, x_in, mgrad,
    f_kept0, f_r10, f_r20, f_rz0, f_kept1, f_r11, f_r21, f_rz1,
    a_sum, a_got, a_r1, a_r2, a_rz,
    q_sum, q_rx, q_ry, q_rz, g_core, g_here, s_own, s_dp, s_mp,
    load_sem, do_send, do_recv, f_send, f_recv, a_send, a_recv, c_send, c_recv,
    q_send, q_recv, g_send, g_recv, s_send, s_recv,
):
    p = Place()
    dp, z, core = p.dp, p.z, p.core
    rows = x_ref.shape[0]
    pairs = v.shape[0]
    k = Back((qa, ka, v, o, cosine, sine, low, va, kt, dk, dv))

    def qkv_to(turn):
        a, b = dp - core + (p.group + turn) % 2, p.quarter
        return a, b, p.stays(a, b)

    def qkv_from(g):
        a, b = dp - core + (z // 2 + g) % 2, 2 * g + z % 2
        return a, b, p.stays(a, b)

    def other_dp(turn):
        return (dp + turn) % 8, z

    def other_mp(turn):
        return dp, (z + turn) % WAYS

    barrier = pltpu.get_barrier_semaphore()
    count = jnp.int32(0)

    def greet(device, skip=None):
        def signal():
            pl.semaphore_signal(barrier, inc=1, device_id=device, device_id_type=MESH)

        if skip is None:
            signal()
            return 1
        pl.when(jnp.logical_not(skip))(signal)
        return 1 - skip.astype(jnp.int32)

    for turn in range(1, 8):
        count += greet(other_dp(turn))
    for turn in range(1, WAYS):
        count += greet(other_mp(turn))
    for m in range(WAYS):
        for a, b, stays in (p.attention_of(m), p.owner_of(m)):
            count += greet((a, b), stays)
    for i in range(2):
        for a, b, stays in (qkv_to(i), qkv_from(i)):
            count += greet((a, b), stays)
    pl.semaphore_wait(barrier, count)

    def head_grad(m, pair, place):
        return Move(
            hg_ref.at[m, pair], do_ref.at[m, pair], do_send.at[m, pair], do_recv.at[m, pair], place
        )

    for pair in range(pairs):
        for m in range(WAYS):
            head_grad(m, pair, p.attention_of(m)).start()

    def half(h):
        kept, r1, r2, rz = ((f_kept0, f_r10, f_r20, f_rz0), (f_kept1, f_r11, f_r21, f_rz1))[h]
        some = pl.ds(h * f_kept0.shape[2], kept.shape[2])
        return Chain(
            p, lambda q, i: sum_ref.at[q, i, some], lambda q, slot, i: kept.at[q, slot],
            r1, r2, rz, f_send.at[h], f_recv.at[h],
        )

    ffn = [half(0), half(1)]
    loads = []

    def load(src, dst):
        copy = pltpu.make_async_copy(src, dst, load_sem.at[len(loads)])
        copy.start()
        loads.append(copy)
        return copy

    def fetch(h, q):
        kept, r1 = (f_kept0, f_r10) if h == 0 else (f_kept1, f_r11)
        some = pl.ds(h * f_kept0.shape[2], kept.shape[2])
        copies = []
        for slot in range(2):
            copies.append(load(sum_ref.at[q, ffn[h].slab(q, slot, False), some], kept.at[q, slot]))
        if q in DONE:
            copies.append(load(r1_ref.at[DONE.index(q), :, some], r1.at[q]))
        return copies

    fetched = {(h, q): fetch(h, q) for q in (0, 2, 1, 3) for h in range(2)}

    def second(h, q):
        for copy in fetched[h, q]:
            copy.wait()
        ffn[h].second(q, q in DONE)

    def third(h, *quarters):
        for q in quarters:
            ffn[h].third(q)

    def line(h, hop, *quarters):
        ffn[h].line(hop, quarters)

    for h in range(2):
        second(h, 0)
        second(h, 2)
        ffn[h].first(1)
        ffn[h].first(3)
    late = [load(normed_ref, normed), load(w_ref, weight), load(x_ref, x_in)]
    late.append(load(mgrad_ref, mgrad))

    low_here = own_first(core, low_ref[...])
    for m in range(WAYS):
        mixed = jnp.concatenate([heads_ref[m, 0], heads_ref[m, 1]], axis=-1)
        value = dot_tn(mixed, low_here).astype(BF)
        h = p.mix(z, m)
        for d in range(value.shape[1] // LANES):
            a_sum[d % 2, h, d // 2] = value[:, d * LANES : (d + 1) * LANES]
    swap = remote(a_sum.at[1], a_got, c_send.at[0], c_recv.at[0], (p.at_c, z))
    swap.start()
    attn_back_begin(0, k)
    swap.wait()
    for q in range(WAYS):
        a_sum[0, q] += a_got[q]
    attn = Chain(
        p, lambda q, i: a_sum.at[0, q, i], lambda q, slot, i: a_sum.at[0, q, i],
        a_r1, a_r2, a_rz, a_send, a_recv,
    )
    for q in range(WAYS):
        attn.first(q)

    def qkv_x(pair, yy):
        at = (p.y if yy else 1 - p.y) * 4 + (1 - p.x) * 2
        return remote(
            q_sum.at[pair, pl.ds(at, 2)], q_rx.at[pair, yy],
            q_send.at[pair, yy], q_recv.at[pair, yy], (p.at_x, z),
        )

    def qkv_y(pair):
        at = (1 - p.y) * 4 + p.x * 2
        return remote(
            q_sum.at[pair, pl.ds(at, 2)], q_ry.at[pair],
            q_send.at[pair, 2], q_recv.at[pair, 2], (p.at_y, z),
        )

    def qkv_z(pair, turn, g, place):
        at = p.y * 4 + p.x * 2 + (p.group + turn) % 2
        return Move(
            q_sum.at[pair, at], q_rz.at[pair, g],
            q_send.at[pair, 3 + turn], q_recv.at[pair, 3 + g], place,
        )

    def qkv_first(pair):
        total = None
        for m in range(WAYS):
            part = dot_tn(low_piece(pair, m, k, rows), normed[m * rows : (m + 1) * rows, :])
            total = part if total is None else total + part
        value = total.astype(BF)
        for d in range(value.shape[1] // LANES):
            q_sum[pair, d] = value[:, d * LANES : (d + 1) * LANES]
        qkv_x(pair, 0).start()
        qkv_x(pair, 1).start()

    def qkv_second(pair):
        qkv_x(pair, 0).wait_recv()
        at = (1 - p.y) * 4 + p.x * 2
        for i in range(2):
            q_sum[pair, at + i] += q_rx[pair, 0, i]
        qkv_y(pair).start()
        qkv_x(pair, 1).wait_recv()
        at = p.y * 4 + p.x * 2
        for i in range(2):
            q_sum[pair, at + i] += q_rx[pair, 1, i]

    def qkv_third(pair):
        qkv_y(pair).wait_recv()
        at = p.y * 4 + p.x * 2
        for i in range(2):
            q_sum[pair, at + i] += q_ry[pair, i]
        for turn in range(2):
            qkv_z(pair, turn, p.group, qkv_to(turn)).start()

    def pair_end():
        attn_back_end(0, k)
        attn_back_begin(1, k)
        for copy in late:
            copy.wait()
        qkv_first(0)

    every = range(WAYS)
    events = {
        1: [(third, 0, 0, 2), (line, 0, 1, 0, 2)],
        2: [(third, 1, 0, 2), (line, 1, 1, 0, 2)],
        3: [(line, 0, 2, 0, 2)],
        4: [(attn.second, q) for q in every],
        5: [(second, 0, 1), (second, 0, 3), (line, 1, 2, 0, 2)],
        6: [(line, 0, 3, 0, 2)] + [(attn.third, q) for q in every] + [(attn.line, 1, every)],
        7: [(line, 1, 3, 0, 2), (attn.line, 2, every)],
        8: [(second, 1, 1), (second, 1, 3), (attn.line, 3, every), (pair_end,)],
        9: [(third, 0, 1, 3), (line, 0, 1, 1, 3)],
        10: [(qkv_second, 0)],
        11: [(line, 0, 2, 1, 3), (third, 1, 1, 3), (line, 1, 1, 1, 3)],
        12: [(qkv_third, 0)],
        13: [(line, 0, 3, 1, 3), (line, 1, 2, 1, 3)],
        15: [(line, 1, 3, 1, 3)],
    }
    steps = v.shape[1] // STEP
    per = rows // STEP

    def body(i, carry):
        for at, todo in events.items():

            @pl.when(i == at)
            def _(todo=todo):
                for what, *args in todo:
                    what(*args)

        pair, step = i // steps, i % steps
        m = step // per

        @pl.when(step % per == 0)
        def _():
            head_grad(m, pair, p.owner_of(0)).wait_recv()

        at = pl.multiple_of((step - m * per) * STEP, STEP)
        attn_back_step(pair, step, do_ref[m, pair, pl.ds(at, STEP), :], k)
        return carry

    lax.fori_loop(0, pairs * steps, body, 0)
    attn_back_end(1, k)

    joined = jnp.concatenate([weight[d] for d in range(weight.shape[0])], axis=-1)

    def piece_grad(m):
        out = None
        for pair in range(pairs):
            at = pair * 3 * LANES
            part = dot_nn(low_piece(pair, m, k, rows), joined[at : at + 3 * LANES, :])
            out = part if out is None else out + part
        return out.astype(BF)

    def to_core(m):
        return remote(
            normed.at[pl.ds((m + 2) * rows, rows)], g_core.at[m],
            g_send.at[m], g_recv.at[m], (p.at_c, z),
        )

    def to_owner(m, place):
        return Move(
            normed.at[pl.ds(m * rows, rows)], g_here.at[m], g_send.at[2 + m], g_recv.at[2 + m], place
        )

    qkv_first(1)
    for m in range(2):
        normed[(m + 2) * rows : (m + 3) * rows, :] = piece_grad(m + 2)
        to_core(m).start()
    for m in range(2):
        own = piece_grad(m)
        to_core(m).wait_recv()
        normed[m * rows : (m + 1) * rows, :] = own + g_core[m]
        to_owner(m, p.owner_of(m)).start()
    qkv_second(1)
    attn.last(attn_ref)
    qkv_third(1)
    cut = f_kept0.shape[2]
    ffn[0].last(ffn_ref.at[:cut])
    ffn[1].last(ffn_ref.at[cut:])
    vhat, scale = norm_stats(x_in[...].astype(F32))
    for pair in range(pairs):
        for g in range(2):
            qkv_z(pair, 0, g, qkv_from(g)).wait_recv()
        qkv_ref[pair] = q_rz[pair, 0].astype(F32) + q_rz[pair, 1].astype(F32)
    for m in range(2):
        to_owner(m, p.attention_of(m)).wait_recv()
    normed_grad = g_here[0].astype(F32) + g_here[1].astype(F32)
    gain_part = jnp.sum(normed_grad * vhat, axis=0, keepdims=True)
    s_own[...] = jnp.concatenate([gain_part, small_ref[1:, :]], axis=0)

    def sum_dp(turn):
        return remote(
            s_own, s_dp.at[turn], s_send.at[turn], s_recv.at[turn], other_dp(turn)
        )

    def sum_mp(turn):
        return remote(
            s_dp.at[0], s_mp.at[turn], s_send.at[8 + turn], s_recv.at[8 + turn], other_mp(turn)
        )

    for turn in range(1, 8):
        sum_dp(turn).start()
    grad_ref[...] = mgrad[...] + norm_back(vhat, scale, gain_ref[...], normed_grad)
    total = s_own[...]
    for turn in range(1, 8):
        sum_dp(turn).wait_recv()
        total += s_dp[turn]
    s_dp[0] = total
    for turn in range(1, WAYS):
        sum_mp(turn).start()
    for turn in range(1, WAYS):
        sum_mp(turn).wait_recv()
        total += s_mp[turn]
    total_ref[...] = total

    for turn in range(1, 8):
        sum_dp(turn).wait_send()
    for turn in range(1, WAYS):
        sum_mp(turn).wait_send()
    for m in range(2):
        to_core(m).wait_send()
        to_owner(m, p.owner_of(m)).wait_send()
    for m in range(WAYS):
        for pair in range(pairs):
            head_grad(m, pair, p.attention_of(m)).wait_send()
    for pair in range(pairs):
        qkv_x(pair, 0).wait_send()
        qkv_x(pair, 1).wait_send()
        qkv_y(pair).wait_send()
        for turn in range(2):
            qkv_z(pair, turn, p.group, qkv_to(turn)).wait_send()
    ffn[0].finish(DONE)
    ffn[1].finish(DONE)
    attn.finish()


def backward_call(heads_grad, ffn_sum, r1, kept, weight, x, middle_grad, low, heads, gain, small):
    normed, cosine, sine, qa, ka, v, o = kept
    rows, model = x.shape
    pairs, tokens, unused = v.shape
    wide, cols3, unused = weight.shape
    units = ffn_sum.shape[2]
    depth = model // WAYS
    third = cols3 // pairs
    part = (units // 32 + 1) * 16
    anywhere = pl.BlockSpec(memory_space=pl.ANY)
    vmem = pl.BlockSpec(memory_space=pltpu.VMEM)
    buf = lambda *shape, kind=BF: pltpu.VMEM(shape, kind)
    sems = lambda *shape: pltpu.SemaphoreType.DMA(shape)
    return pl.pallas_call(
        backward_kernel,
        in_specs=[anywhere] * 7 + [vmem] * 10,
        out_specs=[vmem] * 5,
        out_shape=[
            shape_of((rows, model), F32),
            shape_of((units, LANES), F32),
            shape_of((depth, LANES), F32),
            shape_of((pairs, third, LANES), F32),
            shape_of(small.shape, F32),
        ],
        scratch_shapes=[
            buf(WAYS, pairs, rows, LANES),
            buf(pairs, 3, tokens, LANES),
            buf(2, tokens, LANES),
            buf(2, LANES, tokens),
            buf(tokens, LANES, kind=F32),
            buf(tokens, LANES, kind=F32),
            buf(tokens, model),
            buf(wide, cols3, LANES),
            buf(rows, model),
            buf(rows, model, kind=F32),
            *[
                buf(*lead, cut, LANES)
                for cut in (part, units - part)
                for lead in ((WAYS, 2), (WAYS, 2), (WAYS,), (WAYS + 1,))
            ],
            buf(2, WAYS, wide // 2, depth, LANES),
            buf(WAYS, wide // 2, depth, LANES),
            buf(WAYS, 2, depth, LANES),
            buf(WAYS, depth, LANES),
            buf(WAYS + 1, depth, LANES),
            buf(pairs, wide, third, LANES),
            buf(pairs, 2, 2, third, LANES),
            buf(pairs, 2, third, LANES),
            buf(pairs, 2, third, LANES),
            buf(2, rows, model),
            buf(2, rows, model),
            buf(*small.shape, kind=F32),
            buf(8, *small.shape, kind=F32),
            buf(WAYS, *small.shape, kind=F32),
            sems(26),
            sems(WAYS, pairs),
            sems(WAYS, pairs),
            sems(2, 16),
            sems(2, 17),
            sems(16),
            sems(17),
            sems(1),
            sems(1),
            sems(pairs, 5),
            sems(pairs, 5),
            sems(4),
            sems(4),
            sems(12),
            sems(12),
        ],
        compiler_params=pltpu.CompilerParams(
            collective_id=2, has_side_effects=True, vmem_limit_bytes=62 * 1024 * 1024
        ),
        name="backward",
    )(
        heads_grad, ffn_sum, r1, normed, weight, x, middle_grad, low, heads,
        qa, ka, v, o, cosine, sine, gain, small,
    )


def pick(values, at, axis=0):
    return lax.dynamic_index_in_dim(values, at, axis, keepdims=False)


def flip(values, bit, dps):
    return lax.ppermute(values, "dp", [(i, i ^ bit) for i in range(dps)])


def to_attention(values, m, dps, back=False):
    pairs = []
    for dp in range(dps):
        group = dp % 2
        for t in range(WAYS):
            quarter = t ^ m
            there = (dp - group + ((quarter // 2) ^ group)) * WAYS + 2 * group + quarter % 2
            pairs.append((there, dp * WAYS + t) if back else (dp * WAYS + t, there))
    return lax.ppermute(values, ("dp", "mp"), pairs)


def local(
    sizes,
    layer_input,
    segment_ids,
    grad_out,
    qkv_weight,
    attn_weight,
    inner_weight,
    outer_weight,
    attn_gain,
    mlp_gain,
):
    dps, mps = sizes
    rows, model = layer_input.shape
    head_cols = qkv_weight.shape[2]
    units = inner_weight.shape[2]
    pairs = head_cols // LANES
    wide = model // LANES
    special = dps == wide
    me = lax.axis_index("mp")
    dp = lax.axis_index("dp")
    core = dp % 2
    group = me // 2
    quarter = me ^ (2 * core)
    scalars = jnp.stack([me, core if special else 0, quarter]).astype(jnp.int32)

    def every(values):
        got = lax.all_gather(values.T, "dp", axis=0, tiled=True).T
        got = got.reshape(-1, wide, LANES).transpose(1, 0, 2)
        return lax.all_gather(got, "mp", axis=1)

    qkv_part = qkv_weight.transpose(1, 2, 0).reshape(3, pairs, LANES, -1)
    qkv_part = qkv_part.transpose(1, 0, 2, 3).reshape(3 * head_cols, -1)
    inner_t = inner_weight.transpose(1, 2, 0)
    outer_t = outer_weight.T
    attn_depth = model // mps
    part_a = jnp.concatenate([attn_weight.T, inner_t[0]], axis=0)
    part_b = jnp.concatenate([inner_t[1], outer_t], axis=0)
    mine = segment_ids[0]
    info = jnp.stack([mine, doc_positions(mine)], axis=1).astype(F32)
    info = jnp.pad(info, ((0, 0), (0, LANES - 2))).reshape(WAYS, rows, LANES)
    live_mine = (pick(mine.reshape(WAYS, rows), me) != 0).astype(F32)[:, None]
    if special:
        (pack_a, pack_b), heads, qkv_own, kept = forward_call(
            layer_input, info, attn_gain[None], qkv_part, [part_a, part_b], dps, pairs
        )
    else:
        x_all = jnp.stack([to_attention(layer_input, m, dps) for m in range(WAYS)])
        qkv_all, pack_a, pack_b = every(qkv_part), every(part_a), every(part_b)
        info = jnp.where(group == core, info, flip(info, 1, dps))
        info = jnp.stack([pick(info, quarter ^ m) for m in range(WAYS)])
        kept = alone_call(x_all, info, attn_gain[None], pick(qkv_all, quarter, 1), pairs)
        heads = kept[6].reshape(pairs, WAYS, rows, LANES)
        heads = [to_attention(heads[:, m], m, dps, back=True) for m in range(WAYS)]
        heads = jnp.stack(heads)
    normed, cosine, sine, qa, ka, v, o = kept

    layer_output, middle_grad, middle_low, small, heads_grad, ffn_sum, ffn_got = mlp_call(
        scalars, heads, layer_input, grad_out, mlp_gain[None], live_mine, pack_a, pack_b, special
    )
    if special:
        input_grad, ffn_sum, attn_sum, qkv_sum, small = backward_call(
            heads_grad, ffn_sum, ffn_got, kept, qkv_own, layer_input, middle_grad, middle_low, heads,
            attn_gain[None], small,
        )
        qkv_sum = qkv_sum.reshape(3 * head_cols, -1)
    else:
        lows = []
        for pair in range(pairs):
            grad = [to_attention(heads_grad[m, pair], m, dps) for m in range(WAYS)]
            low = attn_bwd_call(scalars, qa, ka, v, grad, o, cosine, sine, pair)
            lows.append(jnp.concatenate(low, axis=0))
        low = jnp.concatenate(lows, axis=1)
        own = pick(qkv_all, quarter, 1)
        own = jnp.concatenate([own[d] for d in range(wide)], axis=-1)
        normed_grad = dot_nn(low, own).astype(BF).reshape(WAYS, rows, model)
        normed_grad = sum(
            to_attention(normed_grad[m], m, dps, back=True).astype(F32) for m in range(WAYS)
        )

        def scatter(values):
            cut = lax.psum_scatter(values, "mp", scatter_dimension=0)
            return lax.psum_scatter(cut.T, "dp", scatter_dimension=0, tiled=True).T

        slot = (jnp.arange(mps) == quarter)[:, None, None]
        qkv_sum = scatter(jnp.where(slot, dot_tn(low, normed)[None], 0.0))
        mixed = jnp.stack([pick(heads, me ^ h) for h in range(mps)])
        mixed = mixed.transpose(0, 2, 1, 3).reshape(mps, rows, -1)
        attn_sum = scatter(jnp.stack([dot_tn(mixed[h], middle_low) for h in range(mps)]))
        ffn_sum = ffn_sum.reshape(mps, wide, 3 * units, LANES).transpose(0, 2, 1, 3)
        ffn_sum = scatter(ffn_sum.reshape(mps, 3 * units, model).astype(F32))
        vhat, scale = norm_stats(layer_input.astype(F32))
        input_grad = middle_grad + norm_back(vhat, scale, attn_gain, normed_grad)
        small = small.at[0].set(jnp.sum(normed_grad * vhat, axis=0))
        small = lax.psum(small, ("dp", "mp"))
    rms_values = jnp.sqrt(small[2, :4] / (small[2, 4] * model))

    qkv_sum = qkv_sum.reshape(pairs, 3, LANES, -1).transpose(3, 1, 0, 2)
    ffn_sum = ffn_sum.reshape(3, units, -1)
    return (
        layer_output,
        input_grad,
        qkv_sum.reshape(-1, 3, head_cols),
        attn_sum.T,
        ffn_sum[:2].transpose(2, 0, 1),
        ffn_sum[2].T,
        small[0],
        small[1],
        rms_values,
    )


def solution(mesh):
    sizes = (mesh.shape["dp"], mesh.shape["mp"])
    both = ("dp", "mp")
    whole = (P(both, None), P("dp", None, "mp"), P("dp", "mp"))
    return jax.shard_map(
        functools.partial(local, sizes),
        mesh=mesh,
        in_specs=(
            whole[0],
            P("dp", None),
            whole[0],
            whole[1],
            whole[2],
            whole[1],
            whole[2],
            P(),
            P(),
        ),
        out_specs=(
            whole[0],
            whole[0],
            whole[1],
            whole[2],
            whole[1],
            whole[2],
            P(),
            P(),
            P(),
        ),
        check_vma=False,
    )
```

profile of v0, /device:TPU:0, one launch (start us, length us, event | category | flops | bytes accessed | tf_op | source)
XLA Modules:
  0.0 400.1 jit_solution(1674114764779433159)
XLA Ops:
  0.6 0.0 copy-start.3
  0.7 0.6 pad_add_fusion.s_ref
  1.3 0.5 broadcast.27
  1.8 1.4 reduce.5
  3.2 0.9 add_select_fusion
  4.0 0.3 reduce-window.9
  4.3 0.1 slice.54
  4.4 0.1 slice_reduce_fusion
  4.5 0.1 broadcast_maximum_fusion
  4.6 0.7 add_convert_fusion
  5.3 1.0 copy.25
  6.3 1.0 reshape.99
  7.3 0.8 copy.24
  8.1 0.9 copy.26.live_ref
  9.0 1.0 slice_bitcast_fusion.1
  10.0 0.8 pad_maximum_fusion.refs_1_
  10.8 0.7 pad_maximum_fusion.1.refs_0_
  11.5 0.4 copy.29
  11.8 1.0 pad.4.clone
  12.9 139.0 %forward.1 = (bf16[8,4,912,128]{3,2,1,0:T(8,128)(2,1)}, bf16[8,4,1312,128]{3,2,1,0:T(8,128)(2,1)}, bf16[4,2,512,128]{3,2,1,0:T(8,128)(2,1)}, bf16[8,768,128]{2,1...) custom-call(bf16[512,1024]{1,0:T(8,128)(2,1)} %x_ref.5, ...), custom_call_target="tpu_custom_call" | custom-call | tf_op jit(solution)/shard_map/forward/pallas_call | solution.py:779
  151.9 66.9 %mlp.1 = (bf16[512,1024]{1,0:T(8,128)(2,1)}, f32[512,1024]{1,0:T(8,128)}, bf16[512,1024]{1,0:T(8,128)(2,1)}, f32[8,1024]{1,0:T(8,128)}, bf16[4,2,512,128]{3,2,1,...) custom-call(s32[3]{0:T(128)} %pad_add_fusion.s_ref, ...), custom_call_target="tpu_custom_call" | custom-call | flops 30266097664 | bytes 41943040 | tf_op jit(solution)/shard_map/mlp/pallas_call | solution.py:1179
  218.8 167.4 %backward.1 = (f32[512,1024]{1,0:T(8,128)}, f32[1968,128]{1,0:T(8,128)}, f32[256,128]{1,0:T(8,128)}, f32[2,384,128]{2,1,0:T(8,128)}, f32[8,1024]{1,0:T(8,128)}) custom-call(bf16[4,2,512,128]{3,2,1,0:T(8,128)(2,1)} %get-tuple-element.36.hg_ref, bf16[4,4,1968,128]{3,2,1,0:T(8,128)(2,1)} %get-tuple-element.37.sum_ref, ...), custom_call_target="tpu_custom_call" | custom-call | tf_op jit(solution)/shard_map/backward/pallas_call | solution.py:1537
  386.2 1.4 slice.53
  388.2 1.2 sqrt_bitcast_fusion
  389.4 1.2 copy.27
  390.6 1.1 reshape.101
  391.7 1.4 fusion.2
  393.1 1.7 copy.28
  394.8 1.9 slice_bitcast_fusion
  396.7 0.9 slice.47
  397.6 1.0 copy.32
  398.5 1.3 copy.33
  (11 shorter events, 0.1 us)
Async XLA Ops:
  0.6 9.4 %copy-start.3 = (bf16[128,656]{0,1:T(8,128)(2,1)S(1)}, bf16[128,656]{0,1:T(8,128)(2,1)}, u32[]{:S(2)}) copy-start(bf16[128,656]{0,1:T(8,128)(2,1)} %param.15) | copy-start | bytes 503812
  386.2 10.5 %copy-start.2 = (f32[1968,128]{1,0:T(8,128)S(1)}, f32[1968,128]{1,0:T(8,128)}, u32[]{:S(2)}) copy-start(f32[1968,128]{1,0:T(8,128)} %get-tuple-element.53) | copy-start | bytes 3022852
  386.2 11.4 %copy-start.1 = (bf16[512,1024]{1,0:T(8,128)(2,1)S(1)}, bf16[512,1024]{1,0:T(8,128)(2,1)}, u32[]{:S(2)}) copy-start(bf16[512,1024]{1,0:T(8,128)(2,1)} %get-tuple-element.86) | copy-start | bytes 3145732
  394.8 3.7 copy-start
where the time goes:
time: 404 us; the launch traced here: 400 us
  Pallas kernels  373 us (92%)
  local copies, waits for them, and re-layouts  18.6 us (5%)
  other arithmetic  6.59 us (2%)
    pallas_call x1, Pallas kernels, backward_call(): pl.pallas_call(backward_kernel, in_specs=[anywhere] * 7 + [vmem] * 10, ou...  167 us
    pallas_call x1, Pallas kernels, forward_call(): pl.pallas_call(functools.partial(forward_kernel, packs=packs), in_specs=[...  139 us
    pallas_call x1, Pallas kernels, mlp_call(): pl.pallas_call(functools.partial(mlp_kernel, swap=swap), grid_spec=spec,...  66.9 us

commit v1 on v0

--- a/solution.py
+++ b/solution.py
@@ -44,14 +44,6 @@
     mean_u = jnp.mean(u, axis=-1, keepdims=True)
     mean_uv = jnp.mean(u * vhat, axis=-1, keepdims=True)
     return scale * (u - mean_u - vhat * mean_uv)
-
-
-def doc_positions(segment):
-    length = segment.shape[0]
-    places = jnp.arange(length, dtype=jnp.int32)
-    before = jnp.concatenate([jnp.full((1,), -1, jnp.int32), segment[:-1]])
-    starts = jnp.where(segment != before, places, jnp.zeros_like(places))
-    return places - lax.cummax(starts, axis=0)
 
 
 def swap_halves(values):
@@ -113,10 +105,22 @@
 STEP = 256
 
 
-def table_piece(m, info, out):
-    rows = info.shape[0]
+def doc_starts(pieces):
+    number = lax.broadcasted_iota(jnp.int32, (1, LANES), 1).astype(F32)
+    total = jnp.zeros((1, LANES), F32)
+    for piece in pieces:
+        before = jnp.logical_and(piece > 0.0, piece < number)
+        total += jnp.sum(jnp.where(before, 1.0, 0.0), axis=0, keepdims=True)
+    return total
+
+
+def table_piece(m, segment, first, starts, out):
+    rows = segment.shape[0]
     here = slice(m * rows, (m + 1) * rows)
-    segment, position = info[:, 0:1], info[:, 1:2]
+    number = lax.broadcasted_iota(jnp.int32, (1, LANES), 1).astype(F32)
+    start = jnp.sum(jnp.where(segment == number, starts, 0.0), axis=-1, keepdims=True)
+    place = lax.broadcasted_iota(jnp.int32, (rows, 1), 0) + first
+    position = place.astype(F32) - start
     lane = lax.broadcasted_iota(jnp.int32, (1, LANES), 1)
     half = HEAD_DIM // 2
     frequency = jnp.exp((lane % half).astype(F32) * (-2.0 * math.log(ROPE_BASE) / HEAD_DIM))
@@ -131,7 +135,7 @@
     found = jnp.where(same, 1.0, 0.0)
     counted = jnp.where(t < 19, 1.0, 0.0)
     out.kaux[here, :] = jnp.where(t < 16, found, counted).astype(BF)
-    out.live[here, :] = jnp.where(segment != 0.0, 1.0, 0.0)
+    out.live[here, :] = jnp.where(segment[:, 0:1] != 0.0, 1.0, 0.0)
 
 
 def qkv_piece(m, x, gain, weight, out):
@@ -220,10 +224,12 @@
     return outs, scratch
 
 
-def alone_kernel(x_ref, info_ref, gain_ref, w_ref, *refs):
+def alone_kernel(quarter_ref, x_ref, info_ref, gain_ref, w_ref, *refs):
     out = Kept(refs)
+    starts = doc_starts([info_ref[t] for t in range(WAYS)])
     for m in range(WAYS):
-        table_piece(m, info_ref[m], out)
+        t = quarter_ref[0] ^ m
+        table_piece(m, info_ref[t], t * info_ref.shape[1], starts, out)
         qkv_piece(m, x_ref[m], gain_ref[...], side_by_side(w_ref), out)
 
     def body(step, carry):
@@ -234,17 +240,18 @@
     lax.fori_loop(0, out.v.shape[0] * out.v.shape[1] // STEP, body, 0)
 
 
-def alone_call(x, info, gain, weight, pairs):
+def alone_call(quarter, x, info, gain, weight, pairs):
     outs, scratch = kept_shapes(WAYS * x.shape[1], x.shape[2], pairs)
     return pl.pallas_call(
         alone_kernel,
-        in_specs=[pl.BlockSpec(memory_space=pltpu.VMEM)] * 4,
+        in_specs=[pl.BlockSpec(memory_space=pltpu.SMEM)]
+        + [pl.BlockSpec(memory_space=pltpu.VMEM)] * 4,
         out_specs=[pl.BlockSpec(memory_space=pltpu.VMEM)] * len(outs),
         out_shape=outs,
         scratch_shapes=scratch,
         compiler_params=params(),
         name="forward",
-    )(x, info, gain, weight)
+    )(quarter.reshape(1), x, info, gain, weight)
 
 
 def piece_block(m, rows, per):
@@ -364,6 +371,7 @@
 MESH = pl.DeviceIdType.MESH
 UP, DOWN, TO_X, TO_Y, TO_D, CORE_OWN, CORE_X, CORE_Y, CORE_D = range(9)
 FROM_Z, FROM_X, FROM_Y, FROM_D = range(4)
+CHUNKS = 4
 
 
 class Place:
@@ -426,7 +434,8 @@
     kept = Kept((normed, cosine, sine, qa, ka, v, o, q, qaux, kaux, live, scores))
     x_all, w_ref, infos = refs[12:15]
     (
-        sends, recvs, cores, locals_, token_send, token_recv, head_send, head_recv,
+        sends, recvs, cores, locals_, token_send, token_recv, relay_send, info_sem,
+        head_send, head_recv,
         q_send, q_recv, save_sem,
     ) = refs[15:]
     dp, z = lax.axis_index("dp"), lax.axis_index("mp")
@@ -574,24 +583,57 @@
             for kind in range(TO_X, CORE_D + 1):
                 copy(p, kind, s).wait_send()
 
-    def token(m):
+    far = (z // 2 + core) % 2 == 1
+    straight = (z + 1 + core) % 2
+    relays = jnp.logical_and(core == 1, jnp.logical_and(z > 0, z < WAYS - 1))
+    beside = (dp, z + 1 - 2 * (z % 2))
+    cut = x_ref.shape[0] // CHUNKS
+
+    def token(m, c):
         to_dp, to_z, stays = here[m]
-
-        def far():
-            return remote(x_ref, x_all.at[m], token_send.at[m], token_recv.at[m], (to_dp, to_z))
+        some = pl.ds(c * cut, cut)
+        src, dst = x_ref.at[some], x_all.at[m, some]
+
+        def direct():
+            return remote(src, dst, token_send.at[m, c], token_recv.at[m, c], (to_dp, to_z))
 
         def near():
-            return pltpu.make_async_copy(x_ref, x_all.at[m], token_recv.at[m])
-
-        return far, near, stays
-
-    def pass_on(m):
+            return pltpu.make_async_copy(src, dst, token_recv.at[m, c])
+
+        goes = jnp.logical_and(
+            jnp.logical_not(stays), jnp.logical_or(jnp.logical_not(far), straight == m)
+        )
+        return direct, near, stays, goes
+
+    def relay(m, c):
+        some = pl.ds(c * cut, cut)
         return remote(
-            x_all.at[m], x_all.at[m + 2], token_send.at[m + 2], token_recv.at[m + 2], (at_c, z)
+            x_all.at[m, some], x_all.at[1 - m, some],
+            relay_send.at[m, c], token_recv.at[1 - m, c], beside,
         )
 
+    def pass_on(m, c):
+        some = pl.ds(c * cut, cut)
+        return remote(
+            x_all.at[m, some], x_all.at[m + 2, some],
+            token_send.at[m + 2, c], token_recv.at[m + 2, c], (at_c, z),
+        )
+
+    def take_tokens(c):
+        for m in range(2):
+            token(m, c)[0]().wait_recv()
+            pl.when(relays)(lambda m=m: relay(m, c).start())
+            pass_on(m, c).start()
+
+    def early(*chunks):
+        def run():
+            for c in chunks:
+                take_tokens(c)
+
+        pl.when(relays)(run)
+
     def swap_info():
-        return remote(info_ref, infos.at[1], token_send.at[WAYS], token_recv.at[WAYS], (at_c, z))
+        return remote(info_ref, infos.at[1], info_sem.at[0], info_sem.at[1], (at_c, z))
 
     def own_info():
         return pltpu.make_async_copy(info_ref, infos.at[0], locals_.at[packs])
@@ -657,8 +699,11 @@
     q_copy("x", 0, qkv_ref).start()
     q_copy("y", 0, qkv_ref).start()
     own_q().start()
-    for m in range(2):
-        start(token(m))
+    for c in range(CHUNKS):
+        for m in range(2):
+            direct, near, stays, goes = token(m, c)
+            pl.when(stays)(lambda: near().start())
+            pl.when(goes)(lambda: direct().start())
     swap_info().start()
     own_info().start()
     for p in range(packs):
@@ -672,9 +717,12 @@
     q_arrived("z")
     q_copy("x", 1).start()
     q_copy("y", 1).start()
+    early(0)
     away = (group + core) % 2
+    starts = doc_starts([infos[away, t] for t in range(WAYS)])
     for m in range(WAYS):
-        table_piece(m, infos[away, mix(quarter, m)], kept)
+        t = mix(quarter, m)
+        table_piece(m, infos[away, t], t * x_ref.shape[0], starts, kept)
     q_arrived("y", 0)
     q_copy("c").start()
     plane(0, 0)
@@ -683,10 +731,12 @@
     q_arrived("y", 1)
     q_copy("d", 1).start()
     q_copy("cy").start()
+    early(1)
     plane(1, 0)
     q_arrived("d", 0)
     q_arrived("d", 1)
     q_copy("cd").start()
+    early(2)
     reach(0, 1)
     corner(0, 0)
     reach(1, 1)
@@ -696,15 +746,19 @@
     save(0).start()
     save(2).start()
     save(3).start()
-    for m in range(2):
-        token(m)[0]().wait_recv()
-        pass_on(m).start()
+    early(3)
+    @pl.when(jnp.logical_not(relays))
+    def _():
+        for c in range(CHUNKS):
+            take_tokens(c)
+
     for p in range(packs):
         ahead(p, 1)
         plane(p, 1)
     for m in range(WAYS):
         if m >= 2:
-            pass_on(m - 2).wait_recv()
+            for c in range(CHUNKS):
+                pass_on(m - 2, c).wait_recv()
         weight = jnp.concatenate([w_ref[core, d] for d in range(w_ref.shape[1])], axis=-1)
         qkv_piece(m, x_all[m], gain_ref[...], weight, kept)
         if m == 2:
@@ -756,9 +810,12 @@
         for pair in range(pairs):
             head(pair, m, there[m])[0]().wait_recv()
             end_send(head(pair, m, there[m]))
-    for m in range(2):
-        pass_on(m).wait_send()
-        end_send(token(m))
+    for c in range(CHUNKS):
+        for m in range(2):
+            pass_on(m, c).wait_send()
+            direct, near, stays, goes = token(m, c)
+            pl.when(goes)(lambda: direct().wait_send())
+            pl.when(relays)(lambda m=m, c=c: relay(m, c).wait_send())
     for p in range(packs):
         finish(p)
     for kind, i in q_kinds:
@@ -794,8 +851,10 @@
             pltpu.SemaphoreType.DMA((packs, 4, WAYS)),
             pltpu.SemaphoreType.DMA((packs, 4, WAYS)),
             pltpu.SemaphoreType.DMA((packs + 2,)),
-            pltpu.SemaphoreType.DMA((WAYS + 1,)),
-            pltpu.SemaphoreType.DMA((WAYS + 1,)),
+            pltpu.SemaphoreType.DMA((WAYS, CHUNKS)),
+            pltpu.SemaphoreType.DMA((WAYS, CHUNKS)),
+            pltpu.SemaphoreType.DMA((2, CHUNKS)),
+            pltpu.SemaphoreType.DMA((2,)),
             pltpu.SemaphoreType.DMA((WAYS, pairs)),
             pltpu.SemaphoreType.DMA((WAYS, pairs)),
             pltpu.SemaphoreType.DMA((11,)),
@@ -862,14 +921,12 @@
     k.low[pair, 0, here, :] = dq.astype(BF)
 
 
-def attn_back_end(pair, k):
-    chunk = 512
-    for at in range(0, k.dk.shape[0], chunk):
-        some = slice(at, at + chunk)
-        dk = k.dk[some, :]
-        dk = dk * k.cosine[some, :] - swap_halves(dk) * k.sine[some, :]
-        k.low[pair, 1, some, :] = dk.astype(BF)
-        k.low[pair, 2, some, :] = k.dv[some, :].astype(BF)
+def attn_back_end(pair, m, k, rows):
+    some = slice(m * rows, (m + 1) * rows)
+    dk = k.dk[some, :]
+    dk = dk * k.cosine[some, :] - swap_halves(dk) * k.sine[some, :]
+    k.low[pair, 1, some, :] = dk.astype(BF)
+    k.low[pair, 2, some, :] = k.dv[some, :].astype(BF)
 
 
 def low_piece(pair, m, k, rows):
@@ -994,10 +1051,10 @@
 
 
 def mlp_kernel(
-    s_ref, heads_ref, x_ref, g_ref, gain_ref, live_ref, pack_ref, wa_ref, wb_ref,
-    output_ref, mgrad_ref, low_ref, small_ref, hg_ref, sum_ref, r1_ref, *scratch, swap
+    s_ref, heads_ref, x_ref, g_ref, gain_ref, live_ref, pack_ref, qkv_ref, wa_ref, wb_ref,
+    output_ref, mgrad_ref, low_ref, small_ref, hg_ref, sum_ref, r1_ref, w_ref, *scratch, swap
 ):
-    w_attn, middle, inner, mlp, back, grads, load_sem = scratch[:7]
+    w_attn, middle, inner, mlp, back, grads, segment, load_sem = scratch[:8]
     step = pl.program_id(0)
     steps = pl.num_programs(0)
     quarter = turn_of(step)
@@ -1006,21 +1063,37 @@
     z = s_ref[0]
     core = s_ref[1]
     load = pltpu.make_async_copy(pack_ref.at[:, :, :skip], w_attn, load_sem.at[0])
+
+    def alive():
+        return jnp.where(segment[:, 0:1] != 0.0, 1.0, 0.0)
+
     if swap:
-        away, got, send_sem, recv_sem, f_send, f_recv = scratch[7:]
+        away, got, send_sem, recv_sem, f_send, f_recv, w_send, w_recv = scratch[8:]
         p = Place()
-        core = p.core
-        other = (p.at_c, p.z)
+        core, z = p.core, p.z
+        other = (p.at_c, z)
         chain = Chain(
             p, lambda q, i: grads.at[q, i], None, None, None, None, f_send, f_recv
         )
 
+        beside = (p.dp, p.z + 1 - 2 * (p.z % 2))
+
+        def weight_copy(i):
+            src, device = ((qkv_ref, beside), (qkv_ref, other), (w_ref.at[1], other))[i]
+            return remote(src, w_ref.at[i + 1], w_send.at[i], w_recv.at[i], device)
+
+        def weight_own():
+            return pltpu.make_async_copy(qkv_ref, w_ref.at[0], w_send.at[3])
+
         @pl.when(step == 0)
         def _():
             barrier = pltpu.get_barrier_semaphore()
-            for device in (other, (p.at_x, p.z), (p.at_y, p.z)):
+            for device in (other, (p.at_x, p.z), (p.at_y, p.z), beside):
                 pl.semaphore_signal(barrier, inc=1, device_id=device, device_id_type=MESH)
-            pl.semaphore_wait(barrier, 3)
+            pl.semaphore_wait(barrier, 4)
+            weight_copy(0).start()
+            weight_copy(1).start()
+            weight_own().start()
 
         def give(i):
             return remote(
@@ -1051,8 +1124,11 @@
     @pl.when(step == 0)
     def _():
         load.start()
+        load_live = pltpu.make_async_copy(live_ref.at[z], segment, load_sem.at[1 + WAYS])
+        load_live.start()
         tokens = x_ref[...].astype(F32)
         attn_out = jnp.zeros(tokens.shape, F32)
+        load_live.wait()
         load.wait()
         for m in range(WAYS):
             o = jnp.concatenate([heads_ref[m, 0], heads_ref[m, 1]], axis=-1)
@@ -1061,7 +1137,7 @@
         vhat, unused = norm_stats(total)
         middle[...] = total
         inner[...] = (vhat * gain_ref[...]).astype(BF)
-        live = live_ref[...]
+        live = alive()
         lane = lax.broadcasted_iota(jnp.int32, (1, tokens.shape[1]), 1)
         sums = jnp.where(lane == 4, jnp.sum(live), 0.0)
         for i, values in enumerate((tokens, attn_out, total)):
@@ -1086,6 +1162,12 @@
     if swap:
         pl.when(step >= 1)(lambda: take(step - 1))
         pl.when(step >= 2)(lambda: give(step - 2).wait_send())
+
+        @pl.when(step == steps - 1)
+        def _():
+            weight_copy(0).wait_recv()
+            weight_copy(2).start()
+
     x_mine = own_first(core, x)
     g_mine = own_first(core, grad)
     pieces = (dot_nn(d_act, x_mine), dot_nn(d_lin, x_mine), dot_nn(hidden, g_mine))
@@ -1117,8 +1199,6 @@
 
     @pl.when(step == steps - 1)
     def _():
-        if swap:
-            take(step)
         vhat, scale = norm_stats(middle[...])
         into = back[...]
         middle_grad = g_ref[...].astype(F32) + norm_back(vhat, scale, gain_ref[...], into)
@@ -1132,10 +1212,11 @@
         out = mlp[...]
         output_ref[...] = (middle[...] + out).astype(BF)
         lane = lax.broadcasted_iota(jnp.int32, (1, out.shape[1]), 1)
-        square = jnp.sum(live_ref[...] * out * out)
+        square = jnp.sum(alive() * out * out)
         small_ref[2:3, :] = jnp.where(lane == 3, square, small_ref[2:3, :])
         small_ref[1:2, :] = jnp.sum(into * vhat, axis=0, keepdims=True)
         if swap:
+            take(step)
             give(step - 1).wait_send()
             give(step).wait_send()
             for i in range(WAYS):
@@ -1144,9 +1225,13 @@
             for i in range(len(DONE)):
                 for slot in range(2):
                     stage1(i, slot).wait()
-
-
-def mlp_call(scalars, heads, x, grad, gain, live, pack_a, pack_b, swap):
+            weight_copy(0).wait_send()
+            weight_copy(1).wait()
+            weight_copy(2).wait()
+            weight_own().wait()
+
+
+def mlp_call(scalars, heads, x, grad, gain, live, pack_a, pack_b, qkv, swap):
     tokens, model = x.shape
     wide, quarters, depth_a, unused = pack_a.shape
     units = pack_b.shape[2] // 2
@@ -1163,16 +1248,18 @@
         pltpu.VMEM((tokens, model), F32),
         pltpu.VMEM((tokens, model), F32),
         pltpu.VMEM(out if swap else (8, LANES), BF),
-        sems(1 + WAYS),
+        pltpu.VMEM((tokens, LANES), F32),
+        sems(2 + WAYS),
     ]
     if swap:
-        scratch += [pltpu.VMEM((2,) + out[1:], BF)] * 2 + [sems(2), sems(2), sems(6), sems(6)]
+        scratch += [pltpu.VMEM((2,) + out[1:], BF)] * 2
+        scratch += [sems(2), sems(2), sems(6), sems(6), sems(4), sems(3)]
     r1 = (len(DONE), 2, 3 * units, LANES) if swap else (8, LANES)
     spec = pltpu.PrefetchScalarGridSpec(
         num_scalar_prefetch=1,
         grid=(quarters,),
-        in_specs=[whole] * 5 + [anywhere, weight(depth_a), weight(2 * units)],
-        out_specs=[whole] * 5 + [anywhere if swap else whole, anywhere],
+        in_specs=[whole] * 4 + [anywhere] * 3 + [weight(depth_a), weight(2 * units)],
+        out_specs=[whole] * 5 + [anywhere if swap else whole, anywhere, anywhere],
         scratch_shapes=scratch,
     )
     extra = dict(collective_id=1, has_side_effects=True) if swap else {}
@@ -1187,21 +1274,22 @@
             shape_of((WAYS, depth // LANES, tokens, LANES), BF),
             shape_of(out, BF),
             shape_of(r1, BF),
+            shape_of((WAYS,) + qkv.shape if swap else (8, LANES), BF),
         ],
         compiler_params=pltpu.CompilerParams(vmem_limit_bytes=62 * 1024 * 1024, **extra),
         cost_estimate=cost(22 * tokens * model * units * quarters, 40),
         name="mlp",
-    )(scalars, heads, x, grad, gain, live, pack_a, pack_a, pack_b)
+    )(scalars, heads, x, grad, gain, live, pack_a, qkv, pack_a, pack_b)
 
 
 def backward_kernel(
     hg_ref, sum_ref, r1_ref, normed_ref, w_ref, x_ref, mgrad_ref, low_ref, heads_ref,
     qa, ka, v, o, cosine, sine, gain_ref, small_ref,
-    grad_ref, ffn_ref, attn_ref, qkv_ref, total_ref,
-    do_ref, low, va, kt, dk, dv, normed, weight, x_in, mgrad,
+    grad_ref, inner_ref, outer_ref, attn_ref, qkv_ref, gain_a_ref, gain_m_ref, rms_ref,
+    do_ref, low, va, kt, dk, dv, normed, weight, x_in,
     f_kept0, f_r10, f_r20, f_rz0, f_kept1, f_r11, f_r21, f_rz1,
     a_sum, a_got, a_r1, a_r2, a_rz,
-    q_sum, q_rx, q_ry, q_rz, g_core, g_here, s_own, s_dp, s_mp,
+    q_sum, q_rx, q_ry, q_rz, ret, s_own, s_dp, s_mp,
     load_sem, do_send, do_recv, f_send, f_recv, a_send, a_recv, c_send, c_recv,
     q_send, q_recv, g_send, g_recv, s_send, s_recv,
 ):
@@ -1305,16 +1393,19 @@
         second(h, 2)
         ffn[h].first(1)
         ffn[h].first(3)
-    late = [load(normed_ref, normed), load(w_ref, weight), load(x_ref, x_in)]
-    late.append(load(mgrad_ref, mgrad))
-
-    low_here = own_first(core, low_ref[...])
+    low_load = load(low_ref, x_in)
+    late = [load(normed_ref, normed), load(w_ref, weight)]
+    late.append(load(mgrad_ref, grad_ref))
+
+    low_load.wait()
+    low_here = own_first(core, x_in[...])
     for m in range(WAYS):
         mixed = jnp.concatenate([heads_ref[m, 0], heads_ref[m, 1]], axis=-1)
         value = dot_tn(mixed, low_here).astype(BF)
         h = p.mix(z, m)
         for d in range(value.shape[1] // LANES):
             a_sum[d % 2, h, d // 2] = value[:, d * LANES : (d + 1) * LANES]
+    late.append(load(x_ref, x_in))
     swap = remote(a_sum.at[1], a_got, c_send.at[0], c_recv.at[0], (p.at_c, z))
     swap.start()
     attn_back_begin(0, k)
@@ -1379,8 +1470,21 @@
         for turn in range(2):
             qkv_z(pair, turn, p.group, qkv_to(turn)).start()
 
+    def give_back(pair, m, part, place):
+        some = pl.ds(m * rows, rows)
+        if part == 0:
+            src, dst = low.at[pair, 0, some], ret.at[m, pair, 0]
+        else:
+            src, dst = low.at[pair, pl.ds(1, 2), some], ret.at[m, pair, pl.ds(1, 2)]
+        return Move(src, dst, g_send.at[m, pair, part], g_recv.at[m, pair, part], place)
+
+    def finish_pair(pair):
+        for m in range(WAYS):
+            attn_back_end(pair, m, k, rows)
+            give_back(pair, m, 1, p.owner_of(m)).start()
+
     def pair_end():
-        attn_back_end(0, k)
+        finish_pair(0)
         attn_back_begin(1, k)
         for copy in late:
             copy.wait()
@@ -1423,55 +1527,54 @@
 
         at = pl.multiple_of((step - m * per) * STEP, STEP)
         attn_back_step(pair, step, do_ref[m, pair, pl.ds(at, STEP), :], k)
+
+        @pl.when(step % per == per - 1)
+        def _():
+            give_back(pair, m, 0, p.owner_of(m)).start()
+
         return carry
 
     lax.fori_loop(0, pairs * steps, body, 0)
-    attn_back_end(1, k)
-
-    joined = jnp.concatenate([weight[d] for d in range(weight.shape[0])], axis=-1)
-
-    def piece_grad(m):
-        out = None
-        for pair in range(pairs):
-            at = pair * 3 * LANES
-            part = dot_nn(low_piece(pair, m, k, rows), joined[at : at + 3 * LANES, :])
-            out = part if out is None else out + part
-        return out.astype(BF)
-
-    def to_core(m):
-        return remote(
-            normed.at[pl.ds((m + 2) * rows, rows)], g_core.at[m],
-            g_send.at[m], g_recv.at[m], (p.at_c, z),
-        )
-
-    def to_owner(m, place):
-        return Move(
-            normed.at[pl.ds(m * rows, rows)], g_here.at[m], g_send.at[2 + m], g_recv.at[2 + m], place
-        )
-
+    finish_pair(1)
     qkv_first(1)
-    for m in range(2):
-        normed[(m + 2) * rows : (m + 3) * rows, :] = piece_grad(m + 2)
-        to_core(m).start()
-    for m in range(2):
-        own = piece_grad(m)
-        to_core(m).wait_recv()
-        normed[m * rows : (m + 1) * rows, :] = own + g_core[m]
-        to_owner(m, p.owner_of(m)).start()
+
+    def normed_part(pair, m):
+        slot = p.mix(m, 2 * core)
+        at = pair * 3 * LANES
+        w = [weight[slot, d, at : at + 3 * LANES, :] for d in range(weight.shape[1])]
+        grads = jnp.concatenate([ret[m, pair, c] for c in range(3)], axis=-1)
+        return dot_nn(grads, jnp.concatenate(w, axis=-1))
+
+    normed_grad = None
+    for m in range(WAYS):
+        for part in range(2):
+            give_back(0, m, part, p.attention_of(m)).wait_recv()
+        add = normed_part(0, m)
+        normed_grad = add if normed_grad is None else normed_grad + add
     qkv_second(1)
-    attn.last(attn_ref)
+    depth = a_r2.shape[1]
+    attn.last(dv.at[:depth])
+    attn_ref[...] = dv[:depth, :].T
     qkv_third(1)
     cut = f_kept0.shape[2]
-    ffn[0].last(ffn_ref.at[:cut])
-    ffn[1].last(ffn_ref.at[cut:])
+    units = outer_ref.shape[1]
+    ffn[0].last(dk.at[:cut])
+    ffn[1].last(dk.at[cut : 3 * units])
+    inner_ref[0] = dk[:units, :].T
+    inner_ref[1] = dk[units : 2 * units, :].T
+    outer_ref[...] = dk[2 * units : 3 * units, :].T
     vhat, scale = norm_stats(x_in[...].astype(F32))
     for pair in range(pairs):
         for g in range(2):
             qkv_z(pair, 0, g, qkv_from(g)).wait_recv()
-        qkv_ref[pair] = q_rz[pair, 0].astype(F32) + q_rz[pair, 1].astype(F32)
-    for m in range(2):
-        to_owner(m, p.attention_of(m)).wait_recv()
-    normed_grad = g_here[0].astype(F32) + g_here[1].astype(F32)
+        total = q_rz[pair, 0].astype(F32) + q_rz[pair, 1].astype(F32)
+        for c in range(3):
+            part = total[c * LANES : (c + 1) * LANES, :]
+            qkv_ref[c, :, pair * LANES : (pair + 1) * LANES] = part.T
+    for m in range(WAYS):
+        for part in range(2):
+            give_back(1, m, part, p.attention_of(m)).wait_recv()
+        normed_grad += normed_part(1, m)
     gain_part = jnp.sum(normed_grad * vhat, axis=0, keepdims=True)
     s_own[...] = jnp.concatenate([gain_part, small_ref[1:, :]], axis=0)
 
@@ -1487,7 +1590,7 @@
 
     for turn in range(1, 8):
         sum_dp(turn).start()
-    grad_ref[...] = mgrad[...] + norm_back(vhat, scale, gain_ref[...], normed_grad)
+    grad_ref[...] += norm_back(vhat, scale, gain_ref[...], normed_grad)
     total = s_own[...]
     for turn in range(1, 8):
         sum_dp(turn).wait_recv()
@@ -1498,15 +1601,21 @@
     for turn in range(1, WAYS):
         sum_mp(turn).wait_recv()
         total += s_mp[turn]
-    total_ref[...] = total
+    gain_a_ref[...] = total[0:1, :]
+    gain_m_ref[...] = total[1:2, :]
+    squares = total[2:3, :LANES]
+    lane = lax.broadcasted_iota(jnp.int32, squares.shape, 1)
+    count = jnp.sum(jnp.where(lane == 4, squares, 0.0)) * x_ref.shape[1]
+    rms_ref[...] = jnp.sqrt(squares / count)
 
     for turn in range(1, 8):
         sum_dp(turn).wait_send()
     for turn in range(1, WAYS):
         sum_mp(turn).wait_send()
-    for m in range(2):
-        to_core(m).wait_send()
-        to_owner(m, p.owner_of(m)).wait_send()
+    for m in range(WAYS):
+        for pair in range(pairs):
+            for part in range(2):
+                give_back(pair, m, part, p.owner_of(m)).wait_send()
     for m in range(WAYS):
         for pair in range(pairs):
             head_grad(m, pair, p.attention_of(m)).wait_send()
@@ -1525,7 +1634,7 @@
     normed, cosine, sine, qa, ka, v, o = kept
     rows, model = x.shape
     pairs, tokens, unused = v.shape
-    wide, cols3, unused = weight.shape
+    unused, wide, cols3, unused = weight.shape
     units = ffn_sum.shape[2]
     depth = model // WAYS
     third = cols3 // pairs
@@ -1536,14 +1645,17 @@
     sems = lambda *shape: pltpu.SemaphoreType.DMA(shape)
     return pl.pallas_call(
         backward_kernel,
-        in_specs=[anywhere] * 7 + [vmem] * 10,
-        out_specs=[vmem] * 5,
+        in_specs=[anywhere] * 8 + [vmem] * 9,
+        out_specs=[vmem] * 8,
         out_shape=[
             shape_of((rows, model), F32),
-            shape_of((units, LANES), F32),
-            shape_of((depth, LANES), F32),
-            shape_of((pairs, third, LANES), F32),
-            shape_of(small.shape, F32),
+            shape_of((2, LANES, units // 3), F32),
+            shape_of((LANES, units // 3), F32),
+            shape_of((LANES, depth), F32),
+            shape_of((3, LANES, pairs * LANES), F32),
+            shape_of((1, model), F32),
+            shape_of((1, model), F32),
+            shape_of((1, LANES), F32),
         ],
         scratch_shapes=[
             buf(WAYS, pairs, rows, LANES),
@@ -1553,9 +1665,8 @@
             buf(tokens, LANES, kind=F32),
             buf(tokens, LANES, kind=F32),
             buf(tokens, model),
-            buf(wide, cols3, LANES),
+            buf(WAYS, wide, cols3, LANES),
             buf(rows, model),
-            buf(rows, model, kind=F32),
             *[
                 buf(*lead, cut, LANES)
                 for cut in (part, units - part)
@@ -1570,12 +1681,11 @@
             buf(pairs, 2, 2, third, LANES),
             buf(pairs, 2, third, LANES),
             buf(pairs, 2, third, LANES),
-            buf(2, rows, model),
-            buf(2, rows, model),
+            buf(WAYS, pairs, 3, rows, LANES),
             buf(*small.shape, kind=F32),
             buf(8, *small.shape, kind=F32),
             buf(WAYS, *small.shape, kind=F32),
-            sems(26),
+            sems(27),
             sems(WAYS, pairs),
             sems(WAYS, pairs),
             sems(2, 16),
@@ -1586,8 +1696,8 @@
             sems(1),
             sems(pairs, 5),
             sems(pairs, 5),
-            sems(4),
-            sems(4),
+            sems(WAYS, pairs, 2),
+            sems(WAYS, pairs, 2),
             sems(12),
             sems(12),
         ],
@@ -1659,9 +1769,8 @@
     part_a = jnp.concatenate([attn_weight.T, inner_t[0]], axis=0)
     part_b = jnp.concatenate([inner_t[1], outer_t], axis=0)
     mine = segment_ids[0]
-    info = jnp.stack([mine, doc_positions(mine)], axis=1).astype(F32)
-    info = jnp.pad(info, ((0, 0), (0, LANES - 2))).reshape(WAYS, rows, LANES)
-    live_mine = (pick(mine.reshape(WAYS, rows), me) != 0).astype(F32)[:, None]
+    info = jnp.broadcast_to(mine.astype(F32)[:, None], (mine.shape[0], LANES))
+    info = info.reshape(WAYS, rows, LANES)
     if special:
         (pack_a, pack_b), heads, qkv_own, kept = forward_call(
             layer_input, info, attn_gain[None], qkv_part, [part_a, part_b], dps, pairs
@@ -1670,22 +1779,35 @@
         x_all = jnp.stack([to_attention(layer_input, m, dps) for m in range(WAYS)])
         qkv_all, pack_a, pack_b = every(qkv_part), every(part_a), every(part_b)
         info = jnp.where(group == core, info, flip(info, 1, dps))
-        info = jnp.stack([pick(info, quarter ^ m) for m in range(WAYS)])
-        kept = alone_call(x_all, info, attn_gain[None], pick(qkv_all, quarter, 1), pairs)
+        qkv_own = qkv_all
+        kept = alone_call(
+            quarter, x_all, info, attn_gain[None], pick(qkv_all, quarter, 1), pairs)
         heads = kept[6].reshape(pairs, WAYS, rows, LANES)
         heads = [to_attention(heads[:, m], m, dps, back=True) for m in range(WAYS)]
         heads = jnp.stack(heads)
     normed, cosine, sine, qa, ka, v, o = kept
 
-    layer_output, middle_grad, middle_low, small, heads_grad, ffn_sum, ffn_got = mlp_call(
-        scalars, heads, layer_input, grad_out, mlp_gain[None], live_mine, pack_a, pack_b, special
+    outs = mlp_call(
+        scalars, heads, layer_input, grad_out, mlp_gain[None], info, pack_a, pack_b,
+        qkv_own, special,
     )
+    layer_output, middle_grad, middle_low, small, heads_grad, ffn_sum, ffn_got, qkv_whole = outs
     if special:
-        input_grad, ffn_sum, attn_sum, qkv_sum, small = backward_call(
-            heads_grad, ffn_sum, ffn_got, kept, qkv_own, layer_input, middle_grad, middle_low, heads,
+        input_grad, inner_sum, outer_sum, attn_sum, qkv_sum, gain_a, gain_m, rms = backward_call(
+            heads_grad, ffn_sum, ffn_got, kept, qkv_whole, layer_input, middle_grad, middle_low, heads,
             attn_gain[None], small,
         )
-        qkv_sum = qkv_sum.reshape(3 * head_cols, -1)
+        return (
+            layer_output,
+            input_grad,
+            qkv_sum.transpose(1, 0, 2),
+            attn_sum,
+            inner_sum.transpose(1, 0, 2),
+            outer_sum,
+            gain_a[0],
+            gain_m[0],
+            rms[0, :4],
+        )
     else:
         lows = []
         for pair in range(pairs):

time: 404 us -> 376 us (0.931)
  Pallas kernels: 373 us -> 350 us
    pallas_call x1, Pallas kernels: 139 us -> 128 us  [forward_call(): pl.pallas_call(functools.partial(forward_kernel, packs=packs), in_specs=[...]
    pallas_call x1, Pallas kernels: 66.9 us -> 59.1 us  [mlp_call(): pl.pallas_call(functools.partial(mlp_kernel, swap=swap), grid_spec=spec,...]
    unnamed x14 -> x21, local copies, waits for them, and re-layouts: 5.79 us -> 10.1 us
    pallas_call x1, Pallas kernels: 167 us -> 163 us  [backward_call(): pl.pallas_call(backward_kernel, in_specs=[anywhere] * 8 + [vmem] * 9, out...]
where the time goes in v1:
time: 376 us; the launch traced here: 370 us
  Pallas kernels  350 us (93%)
  local copies, waits for them, and re-layouts  15.5 us (4%)
    pallas_call x1, Pallas kernels, backward_call(): pl.pallas_call(backward_kernel, in_specs=[anywhere] * 8 + [vmem] * 9, out...  163 us
    pallas_call x1, Pallas kernels, forward_call(): pl.pallas_call(functools.partial(forward_kernel, packs=packs), in_specs=[...  128 us
    pallas_call x1, Pallas kernels, mlp_call(): pl.pallas_call(functools.partial(mlp_kernel, swap=swap), grid_spec=spec,...  59.1 us
    unnamed x21, local copies, waits for them, and re-layouts  10.1 us

profile of v1, /device:TPU:0, one launch (start us, length us, event | category | flops | bytes accessed | tf_op | source)
XLA Modules:
  0.0 370.2 jit_solution(8946039416070945165)
XLA Ops:
  0.7 0.6 pad_add_fusion.s_ref
  1.2 0.7 convert_reduce_fusion
  2.0 1.0 copy.19
  2.9 1.0 reshape.36
  3.9 0.8 copy.18
  4.8 1.0 slice_bitcast_fusion
  5.8 1.7 pad_maximum_fusion.refs_1_
  7.4 0.7 pad_maximum_fusion.1.refs_0_
  8.1 1.3 broadcast_in_dim.6.info_ref.live_ref
  9.5 127.7 %forward.1 = (bf16[8,4,912,128]{3,2,1,0:T(8,128)(2,1)}, bf16[8,4,1312,128]{3,2,1,0:T(8,128)(2,1)}, bf16[4,2,512,128]{3,2,1,0:T(8,128)(2,1)}, bf16[8,768,128]{2,1...) custom-call(bf16[512,1024]{1,0:T(8,128)(2,1)} %x_ref.5, ...), custom_call_target="tpu_custom_call" | custom-call | tf_op jit(solution)/shard_map/forward/pallas_call | solution.py:836
  137.1 59.1 %mlp.1 = (bf16[512,1024]{1,0:T(8,128)(2,1)}, f32[512,1024]{1,0:T(8,128)}, bf16[512,1024]{1,0:T(8,128)(2,1)}, f32[8,1024]{1,0:T(8,128)}, bf16[4,2,512,128]{3,2,1,...) custom-call(s32[3]{0:T(128)} %pad_add_fusion.s_ref, ...), custom_call_target="tpu_custom_call" | custom-call | flops 30266097664 | bytes 41943040 | tf_op jit(solution)/shard_map/mlp/pallas_call | solution.py:1266
  196.2 163.1 %backward.1 = (f32[512,1024]{1,0:T(8,128)}, f32[2,128,656]{2,1,0:T(8,128)}, f32[128,656]{1,0:T(8,128)}, f32[128,256]{1,0:T(8,128)}, f32[3,128,256]{2,1,0:T(8,128...) custom-call(bf16[4,2,512,128]{3,2,1,0:T(8,128)(2,1)} %get-tuple-element.41.hg_ref, ...), custom_call_target="tpu_custom_call" | custom-call | tf_op jit(solution)/shard_map/backward/pallas_call | solution.py:1646
  359.4 0.0 copy-start.1
  359.4 1.2 slice_bitcast_fusion.2
  360.5 0.0 copy-start
  360.5 2.0 copy.21
  362.6 2.2 copy.20
  364.8 0.0 copy-done.1
  364.8 1.0 copy.28
  365.8 0.0 copy-done
  365.8 0.0 copy-start.2
  365.8 0.0 copy-start.3
  365.8 0.0 copy-start.4
  365.8 1.3 copy.29
  367.1 0.0 copy-done.2
  367.1 0.7 copy.30
  367.9 0.0 copy-done.3
  367.9 0.7 copy.31
  368.6 0.0 copy-done.5
  368.6 0.6 copy.32
  369.2 0.0 copy-done.4
  369.2 0.6 copy.33
  (2 shorter events, 0.0 us)
Async XLA Ops:
  359.4 5.5 %copy-start.1 = (bf16[512,1024]{1,0:T(8,128)(2,1)S(1)}, bf16[512,1024]{1,0:T(8,128)(2,1)}, u32[]{:S(2)}) copy-start(bf16[512,1024]{1,0:T(8,128)(2,1)} %get-tuple-element.83) | copy-start | bytes 3145732
  360.5 5.3 %copy-start = (f32[512,1024]{1,0:T(8,128)S(1)}, f32[512,1024]{1,0:T(8,128)}, u32[]{:S(2)}) copy-start(f32[512,1024]{1,0:T(8,128)} %get-tuple-element.84) | copy-start | bytes 6291460
  365.8 1.3 copy-start.2
  365.8 2.1 copy-start.3
  365.8 2.7 copy-start.5
  365.8 3.3 copy-start.4

commit v2 on v1

--- a/solution.py
+++ b/solution.py
@@ -769,12 +769,15 @@
     save(5).start()
 
     events = {
-        1: [(line, 1, 2), (corner, 1, 1)],
-        4: [(line, 0, 3), (plane, 0, 2)],
-        7: [(line, 1, 3), (plane, 1, 2)],
+        1: [(line, 1, 2)],
+        2: [(line, 0, 3), (corner, 1, 1)],
+        4: [(plane, 0, 2)],
+        5: [(line, 1, 3)],
+        7: [(plane, 1, 2)],
         9: [(corner, 0, 2)],
         11: [(plane, 0, 3)],
         13: [(corner, 1, 2)],
+        15: [(plane, 1, 3)],
     }
     steps = kept.v.shape[1] // STEP
     pairs = kept.v.shape[0]
@@ -801,7 +804,6 @@
         return carry
 
     lax.fori_loop(0, pairs * steps, body, 0)
-    plane(1, 3)
     corner(0, 3)
     corner(1, 3)
     for p in range(packs):
@@ -1391,8 +1393,6 @@
     for h in range(2):
         second(h, 0)
         second(h, 2)
-        ffn[h].first(1)
-        ffn[h].first(3)
     low_load = load(low_ref, x_in)
     late = [load(normed_ref, normed), load(w_ref, weight)]
     late.append(load(mgrad_ref, grad_ref))
@@ -1416,8 +1416,6 @@
         p, lambda q, i: a_sum.at[0, q, i], lambda q, slot, i: a_sum.at[0, q, i],
         a_r1, a_r2, a_rz, a_send, a_recv,
     )
-    for q in range(WAYS):
-        attn.first(q)
 
     def qkv_x(pair, yy):
         at = (p.y if yy else 1 - p.y) * 4 + (1 - p.x) * 2
@@ -1492,20 +1490,18 @@
 
     every = range(WAYS)
     events = {
-        1: [(third, 0, 0, 2), (line, 0, 1, 0, 2)],
-        2: [(third, 1, 0, 2), (line, 1, 1, 0, 2)],
-        3: [(line, 0, 2, 0, 2)],
-        4: [(attn.second, q) for q in every],
-        5: [(second, 0, 1), (second, 0, 3), (line, 1, 2, 0, 2)],
-        6: [(line, 0, 3, 0, 2)] + [(attn.third, q) for q in every] + [(attn.line, 1, every)],
-        7: [(line, 1, 3, 0, 2), (attn.line, 2, every)],
-        8: [(second, 1, 1), (second, 1, 3), (attn.line, 3, every), (pair_end,)],
-        9: [(third, 0, 1, 3), (line, 0, 1, 1, 3)],
+        1: [(third, 0, 0, 2), (ffn[0].first, 1), (ffn[0].first, 3), (line, 0, 1, 0, 2)],
+        3: [(third, 1, 0, 2), (line, 1, 1, 0, 2)],
+        4: [(line, 0, 2, 0, 2), (second, 0, 1), (second, 0, 3), (ffn[1].first, 1), (ffn[1].first, 3)],
+        6: [(line, 1, 2, 0, 2)] + [(attn.first, q) for q in every],
+        7: [(third, 0, 1, 3), (line, 0, 1, 1, 3), (line, 0, 3, 0, 2)],
+        8: [(second, 1, 1), (second, 1, 3), (pair_end,)],
+        9: [(line, 1, 3, 0, 2), (line, 0, 2, 1, 3)] + [(attn.second, q) for q in every],
         10: [(qkv_second, 0)],
-        11: [(line, 0, 2, 1, 3), (third, 1, 1, 3), (line, 1, 1, 1, 3)],
+        11: [(line, 0, 3, 1, 3), (third, 1, 1, 3), (line, 1, 1, 1, 3)] + [(attn.third, q) for q in every] + [(attn.line, 1, every)],
         12: [(qkv_third, 0)],
-        13: [(line, 0, 3, 1, 3), (line, 1, 2, 1, 3)],
-        15: [(line, 1, 3, 1, 3)],
+        13: [(line, 1, 2, 1, 3), (attn.line, 2, every)],
+        15: [(line, 1, 3, 1, 3), (attn.line, 3, every)],
     }
     steps = v.shape[1] // STEP
     per = rows // STEP

time: 376 us -> 358 us (0.952)
  Pallas kernels: 350 us -> 333 us
    pallas_call x1, Pallas kernels: 163 us -> 148 us  [backward_call(): pl.pallas_call(backward_kernel, in_specs=[anywhere] * 8 + [vmem] * 9, out...]
where the time goes in v2:
time: 358 us; the launch traced here: 353 us
  Pallas kernels  333 us (93%)
  local copies, waits for them, and re-layouts  15.5 us (4%)
  other arithmetic  3.68 us (1%)
    pallas_call x1, Pallas kernels, backward_call(): pl.pallas_call(backward_kernel, in_specs=[anywhere] * 8 + [vmem] * 9, out...  148 us
    pallas_call x1, Pallas kernels, forward_call(): pl.pallas_call(functools.partial(forward_kernel, packs=packs), in_specs=[...  126 us
    pallas_call x1, Pallas kernels, mlp_call(): pl.pallas_call(functools.partial(mlp_kernel, swap=swap), grid_spec=spec,...  58.6 us
    unnamed x21, local copies, waits for them, and re-layouts  10.1 us

profile of v2, /device:TPU:0, one launch (start us, length us, event | category | flops | bytes accessed | tf_op | source)
XLA Modules:
  0.0 352.9 jit_solution(13912067828830933998)
XLA Ops:
  0.7 0.6 pad_add_fusion.s_ref
  1.2 0.7 convert_reduce_fusion
  2.0 1.0 copy.19
  2.9 1.0 reshape.36
  3.9 0.8 copy.18
  4.8 1.0 slice_bitcast_fusion
  5.8 1.7 pad_maximum_fusion.refs_1_
  7.4 0.7 pad_maximum_fusion.1.refs_0_
  8.1 1.3 broadcast_in_dim.6.info_ref.live_ref
  9.5 126.2 %forward.1 = (bf16[8,4,912,128]{3,2,1,0:T(8,128)(2,1)}, bf16[8,4,1312,128]{3,2,1,0:T(8,128)(2,1)}, bf16[4,2,512,128]{3,2,1,0:T(8,128)(2,1)}, bf16[8,768,128]{2,1...) custom-call(bf16[512,1024]{1,0:T(8,128)(2,1)} %x_ref.5, ...), custom_call_target="tpu_custom_call" | custom-call | tf_op jit(solution)/shard_map/forward/pallas_call | solution.py:838
  135.7 58.6 %mlp.1 = (bf16[512,1024]{1,0:T(8,128)(2,1)}, f32[512,1024]{1,0:T(8,128)}, bf16[512,1024]{1,0:T(8,128)(2,1)}, f32[8,1024]{1,0:T(8,128)}, bf16[4,2,512,128]{3,2,1,...) custom-call(s32[3]{0:T(128)} %pad_add_fusion.s_ref, ...), custom_call_target="tpu_custom_call" | custom-call | flops 30266097664 | bytes 41943040 | tf_op jit(solution)/shard_map/mlp/pallas_call | solution.py:1268
  194.3 147.7 %backward.1 = (f32[512,1024]{1,0:T(8,128)}, f32[2,128,656]{2,1,0:T(8,128)}, f32[128,656]{1,0:T(8,128)}, f32[128,256]{1,0:T(8,128)}, f32[3,128,256]{2,1,0:T(8,128...) custom-call(bf16[4,2,512,128]{3,2,1,0:T(8,128)(2,1)} %get-tuple-element.41.hg_ref, ...), custom_call_target="tpu_custom_call" | custom-call | tf_op jit(solution)/shard_map/backward/pallas_call | solution.py:1642
  342.1 0.0 copy-start.1
  342.1 1.2 slice_bitcast_fusion.2
  343.2 0.0 copy-start
  343.2 2.0 copy.21
  345.3 2.2 copy.20
  347.5 0.0 copy-done.1
  347.5 1.0 copy.28
  348.5 0.0 copy-done
  348.5 0.0 copy-start.2
  348.5 0.0 copy-start.3
  348.5 0.0 copy-start.4
  348.5 1.3 copy.29
  349.8 0.0 copy-done.2
  349.8 0.7 copy.30
  350.6 0.0 copy-done.3
  350.6 0.7 copy.31
  351.2 0.0 copy-done.5
  351.2 0.6 copy.32
  351.8 0.0 copy-done.4
  351.8 0.6 copy.33
  (2 shorter events, 0.0 us)
Async XLA Ops:
  342.1 5.5 %copy-start.1 = (bf16[512,1024]{1,0:T(8,128)(2,1)S(1)}, bf16[512,1024]{1,0:T(8,128)(2,1)}, u32[]{:S(2)}) copy-start(bf16[512,1024]{1,0:T(8,128)(2,1)} %get-tuple-element.83) | copy-start | bytes 3145732
  343.2 5.3 %copy-start = (f32[512,1024]{1,0:T(8,128)S(1)}, f32[512,1024]{1,0:T(8,128)}, u32[]{:S(2)}) copy-start(f32[512,1024]{1,0:T(8,128)} %get-tuple-element.84) | copy-start | bytes 6291460
  348.5 1.3 copy-start.2
  348.5 2.1 copy-start.3
  348.5 2.7 copy-start.5
  348.5 3.3 copy-start.4

commit v3 on v2

--- a/solution.py
+++ b/solution.py
@@ -1492,16 +1492,17 @@
     events = {
         1: [(third, 0, 0, 2), (ffn[0].first, 1), (ffn[0].first, 3), (line, 0, 1, 0, 2)],
         3: [(third, 1, 0, 2), (line, 1, 1, 0, 2)],
-        4: [(line, 0, 2, 0, 2), (second, 0, 1), (second, 0, 3), (ffn[1].first, 1), (ffn[1].first, 3)],
+        4: [(line, 0, 2, 0, 2)],
+        5: [(second, 0, 1), (second, 0, 3), (ffn[1].first, 1), (ffn[1].first, 3)],
         6: [(line, 1, 2, 0, 2)] + [(attn.first, q) for q in every],
-        7: [(third, 0, 1, 3), (line, 0, 1, 1, 3), (line, 0, 3, 0, 2)],
-        8: [(second, 1, 1), (second, 1, 3), (pair_end,)],
-        9: [(line, 1, 3, 0, 2), (line, 0, 2, 1, 3)] + [(attn.second, q) for q in every],
-        10: [(qkv_second, 0)],
-        11: [(line, 0, 3, 1, 3), (third, 1, 1, 3), (line, 1, 1, 1, 3)] + [(attn.third, q) for q in every] + [(attn.line, 1, every)],
-        12: [(qkv_third, 0)],
-        13: [(line, 1, 2, 1, 3), (attn.line, 2, every)],
-        15: [(line, 1, 3, 1, 3), (attn.line, 3, every)],
+        7: [(line, 0, 3, 0, 2)],
+        8: [(pair_end,), (third, 0, 1, 3)],
+        9: [(line, 0, 1, 1, 3), (second, 1, 1), (second, 1, 3), (line, 1, 3, 0, 2)],
+        10: [(attn.second, q) for q in every],
+        11: [(qkv_second, 0), (line, 0, 2, 1, 3)] + [(attn.third, q) for q in every] + [(attn.line, 1, every)],
+        12: [(third, 1, 1, 3)],
+        13: [(qkv_third, 0), (line, 0, 3, 1, 3), (line, 1, 1, 1, 3), (attn.line, 2, every)],
+        15: [(line, 1, 2, 1, 3), (attn.line, 3, every)],
     }
     steps = v.shape[1] // STEP
     per = rows // STEP
@@ -1548,6 +1549,7 @@
         add = normed_part(0, m)
         normed_grad = add if normed_grad is None else normed_grad + add
     qkv_second(1)
+    line(1, 3, 1, 3)
     depth = a_r2.shape[1]
     attn.last(dv.at[:depth])
     attn_ref[...] = dv[:depth, :].T

time: 358 us -> 357 us (level)
  no operation moved by 1% of the time
where the time goes in v3:
time: 357 us; the launch traced here: 352 us
  Pallas kernels  332 us (93%)
  local copies, waits for them, and re-layouts  15.5 us (4%)
  other arithmetic  3.68 us (1%)
    pallas_call x1, Pallas kernels, backward_call(): pl.pallas_call(backward_kernel, in_specs=[anywhere] * 8 + [vmem] * 9, out...  147 us
    pallas_call x1, Pallas kernels, forward_call(): pl.pallas_call(functools.partial(forward_kernel, packs=packs), in_specs=[...  126 us
    pallas_call x1, Pallas kernels, mlp_call(): pl.pallas_call(functools.partial(mlp_kernel, swap=swap), grid_spec=spec,...  58.6 us
    unnamed x21, local copies, waits for them, and re-layouts  10.1 us

profile of v3, /device:TPU:0, one launch (start us, length us, event | category | flops | bytes accessed | tf_op | source)
XLA Modules:
  0.0 351.9 jit_solution(3518455638623680309)
XLA Ops:
  0.7 0.6 pad_add_fusion.s_ref
  1.2 0.7 convert_reduce_fusion
  2.0 1.0 copy.19
  2.9 1.0 reshape.36
  3.9 0.8 copy.18
  4.8 1.0 slice_bitcast_fusion
  5.8 1.7 pad_maximum_fusion.refs_1_
  7.4 0.7 pad_maximum_fusion.1.refs_0_
  8.1 1.3 broadcast_in_dim.6.info_ref.live_ref
  9.5 126.2 %forward.1 = (bf16[8,4,912,128]{3,2,1,0:T(8,128)(2,1)}, bf16[8,4,1312,128]{3,2,1,0:T(8,128)(2,1)}, bf16[4,2,512,128]{3,2,1,0:T(8,128)(2,1)}, bf16[8,768,128]{2,1...) custom-call(bf16[512,1024]{1,0:T(8,128)(2,1)} %x_ref.5, ...), custom_call_target="tpu_custom_call" | custom-call | tf_op jit(solution)/shard_map/forward/pallas_call | solution.py:838
  135.7 58.6 %mlp.1 = (bf16[512,1024]{1,0:T(8,128)(2,1)}, f32[512,1024]{1,0:T(8,128)}, bf16[512,1024]{1,0:T(8,128)(2,1)}, f32[8,1024]{1,0:T(8,128)}, bf16[4,2,512,128]{3,2,1,...) custom-call(s32[3]{0:T(128)} %pad_add_fusion.s_ref, ...), custom_call_target="tpu_custom_call" | custom-call | flops 30266097664 | bytes 41943040 | tf_op jit(solution)/shard_map/mlp/pallas_call | solution.py:1268
  194.3 146.8 %backward.1 = (f32[512,1024]{1,0:T(8,128)}, f32[2,128,656]{2,1,0:T(8,128)}, f32[128,656]{1,0:T(8,128)}, f32[128,256]{1,0:T(8,128)}, f32[3,128,256]{2,1,0:T(8,128...) custom-call(bf16[4,2,512,128]{3,2,1,0:T(8,128)(2,1)} %get-tuple-element.41.hg_ref, ...), custom_call_target="tpu_custom_call" | custom-call | tf_op jit(solution)/shard_map/backward/pallas_call | solution.py:1644
  341.1 0.0 copy-start.1
  341.1 1.2 slice_bitcast_fusion.2
  342.3 0.0 copy-start
  342.3 2.0 copy.21
  344.3 2.2 copy.20
  346.6 0.0 copy-done.1
  346.6 1.0 copy.28
  347.5 0.0 copy-done
  347.5 0.0 copy-start.2
  347.5 0.0 copy-start.3
  347.6 0.0 copy-start.4
  347.6 1.3 copy.29
  348.9 0.0 copy-done.2
  348.9 0.7 copy.30
  349.6 0.0 copy-done.3
  349.6 0.7 copy.31
  350.3 0.0 copy-done.5
  350.3 0.6 copy.32
  350.9 0.0 copy-done.4
  350.9 0.6 copy.33
  (2 shorter events, 0.0 us)
Async XLA Ops:
  341.1 5.5 %copy-start.1 = (bf16[512,1024]{1,0:T(8,128)(2,1)S(1)}, bf16[512,1024]{1,0:T(8,128)(2,1)}, u32[]{:S(2)}) copy-start(bf16[512,1024]{1,0:T(8,128)(2,1)} %get-tuple-element.83) | copy-start | bytes 3145732
  342.3 5.3 %copy-start = (f32[512,1024]{1,0:T(8,128)S(1)}, f32[512,1024]{1,0:T(8,128)}, u32[]{:S(2)}) copy-start(f32[512,1024]{1,0:T(8,128)} %get-tuple-element.84) | copy-start | bytes 6291460
  347.5 1.3 copy-start.2
  347.5 2.1 copy-start.3
  347.5 2.7 copy-start.5
  347.6 3.3 copy-start.4

commit v4 on v3

--- a/solution.py
+++ b/solution.py
@@ -1752,7 +1752,9 @@
     core = dp % 2
     group = me // 2
     quarter = me ^ (2 * core)
-    scalars = jnp.stack([me, core if special else 0, quarter]).astype(jnp.int32)
+    scalars = jnp.zeros((3,), jnp.int32)
+    if not special:
+        scalars = jnp.stack([me, 0, quarter]).astype(jnp.int32)
 
     def every(values):
         got = lax.all_gather(values.T, "dp", axis=0, tiled=True).T

time: 357 us -> 357 us (level)
  no operation moved by 1% of the time
where the time goes in v4:
time: 357 us; the launch traced here: 352 us
  Pallas kernels  332 us (93%)
  local copies, waits for them, and re-layouts  16 us (4%)
    pallas_call x1, Pallas kernels, backward_call(): pl.pallas_call(backward_kernel, in_specs=[anywhere] * 8 + [vmem] * 9, out...  147 us
    pallas_call x1, Pallas kernels, forward_call(): pl.pallas_call(functools.partial(forward_kernel, packs=packs), in_specs=[...  126 us
    pallas_call x1, Pallas kernels, mlp_call(): pl.pallas_call(functools.partial(mlp_kernel, swap=swap), grid_spec=spec,...  58.6 us
    unnamed x21, local copies, waits for them, and re-layouts  10.1 us

profile of v4, /device:TPU:0, one launch (start us, length us, event | category | flops | bytes accessed | tf_op | source)
XLA Modules:
  0.0 351.8 jit_solution(17441811922165786439)
XLA Ops:
  0.6 0.7 convert_reduce_fusion
  1.4 1.0 copy.19
  2.3 1.0 reshape.36
  3.3 0.8 copy.18
  4.2 1.0 slice_bitcast_fusion
  5.2 1.7 pad_maximum_fusion.refs_1_
  6.8 0.7 pad_maximum_fusion.1.refs_0_
  7.6 1.3 broadcast_in_dim.6.info_ref.live_ref
  8.9 126.2 %forward.1 = (bf16[8,4,912,128]{3,2,1,0:T(8,128)(2,1)}, bf16[8,4,1312,128]{3,2,1,0:T(8,128)(2,1)}, bf16[4,2,512,128]{3,2,1,0:T(8,128)(2,1)}, bf16[8,768,128]{2,1...) custom-call(bf16[512,1024]{1,0:T(8,128)(2,1)} %x_ref.5, ...), custom_call_target="tpu_custom_call" | custom-call | tf_op jit(solution)/shard_map/forward/pallas_call | solution.py:838
  135.1 0.5 broadcast_1_s_ref.2.s_ref
  135.6 58.6 %mlp.1 = (bf16[512,1024]{1,0:T(8,128)(2,1)}, f32[512,1024]{1,0:T(8,128)}, bf16[512,1024]{1,0:T(8,128)(2,1)}, f32[8,1024]{1,0:T(8,128)}, bf16[4,2,512,128]{3,2,1,...) custom-call(s32[3]{0:T(128)} %broadcast_1_s_ref.2.s_ref, ...), custom_call_target="tpu_custom_call" | custom-call | flops 30266097664 | bytes 41943040 | tf_op jit(solution)/shard_map/mlp/pallas_call | solution.py:1268
  194.2 146.8 %backward.1 = (f32[512,1024]{1,0:T(8,128)}, f32[2,128,656]{2,1,0:T(8,128)}, f32[128,656]{1,0:T(8,128)}, f32[128,256]{1,0:T(8,128)}, f32[3,128,256]{2,1,0:T(8,128...) custom-call(bf16[4,2,512,128]{3,2,1,0:T(8,128)(2,1)} %get-tuple-element.41.hg_ref, ...), custom_call_target="tpu_custom_call" | custom-call | tf_op jit(solution)/shard_map/backward/pallas_call | solution.py:1644
  341.0 0.0 copy-start.1
  341.0 1.2 slice_bitcast_fusion.2
  342.2 0.0 copy-start
  342.2 2.0 copy.21
  344.2 2.2 copy.20
  346.5 0.0 copy-done.1
  346.5 1.0 copy.28
  347.4 0.0 copy-done
  347.4 0.0 copy-start.2
  347.4 0.0 copy-start.3
  347.5 0.0 copy-start.4
  347.5 1.3 copy.29
  348.8 0.0 copy-done.2
  348.8 0.7 copy.30
  349.5 0.0 copy-done.3
  349.5 0.7 copy.31
  350.2 0.0 copy-done.5
  350.2 0.6 copy.32
  350.8 0.0 copy-done.4
  350.8 0.6 copy.33
  (2 shorter events, 0.0 us)
Async XLA Ops:
  341.0 5.5 %copy-start.1 = (bf16[512,1024]{1,0:T(8,128)(2,1)S(1)}, bf16[512,1024]{1,0:T(8,128)(2,1)}, u32[]{:S(2)}) copy-start(bf16[512,1024]{1,0:T(8,128)(2,1)} %get-tuple-element.83) | copy-start | bytes 3145732
  342.2 5.3 %copy-start = (f32[512,1024]{1,0:T(8,128)S(1)}, f32[512,1024]{1,0:T(8,128)}, u32[]{:S(2)}) copy-start(f32[512,1024]{1,0:T(8,128)} %get-tuple-element.84) | copy-start | bytes 6291460
  347.4 1.3 copy-start.2
  347.4 2.1 copy-start.3
  347.4 2.7 copy-start.5
  347.5 3.3 copy-start.4
